TPU v7x, 128 devices: a whole 4x4x4 slice. The times are simulated.
128 devices in a mesh: section: 2 (over x_hi), dp: 16 (over z, y), mp: 4 (over x_lo, core).
Axes of the slice: x: 4 (x_hi: 2, x_lo: 2; x = x_hi * 2 + x_lo), y: 4, z: 4, core: 2. Of those that a mesh axis runs over, the one named last changes fastest.
Arguments:
- text_feats: bfloat16 [16384, 512], P('dp'), may hold values from -48 to 48
- image_feats: bfloat16 [16384, 512], P(('dp', 'mp')), may hold values from -48 to 48
- logit_scale: float32 [1], replicated, may hold values from 10 to 320
- layer_inputs: bfloat16 [2, 16384, 512], P('section', 'dp'), may hold values from -6 to 6
- w_in: bfloat16 [2, 512, 2048], P('section', None, 'mp'), may hold values from -0.25 to 0.25
- w_out: bfloat16 [2, 2048, 512], P('section', 'mp'), may hold values from -0.125 to 0.125
Outputs:
- image_grad: bfloat16 [16384, 512], P(('dp', 'mp'))
- input_grad: bfloat16 [16384, 512], P('dp', 'section')
- w_in_grad: float32 [2, 512, 2048], P('section', 'dp', 'mp')
- w_out_grad_t: float32 [2, 512, 2048], P('section', 'dp', 'mp')
All inputs are finite; a program needn't handle non-finite values.
Results may differ from a plain program's by a relative error of at most 0.017.
Values may be sent and summed in bfloat16 or wider, within the bound.
A program may use at most 128 MiB of HBM per device.

v0:
```python
import jax
import jax.numpy as jnp
from jax import lax
from jax.experimental import pallas as pl
from jax.experimental.pallas import tpu as pltpu
from jax.sharding import PartitionSpec as P

MESH = pl.DeviceIdType.MESH
F32 = jnp.float32
BF16 = jnp.bfloat16
GELU = 1.702
LANES = 128
PIECES = 4


def unit_rows(values):
    wide = values.astype(F32)
    length = jnp.sqrt(jnp.sum(wide * wide, axis=1, keepdims=True) + 1.0)
    return (wide / length, length)


def unit_backward(unit, length, grad_unit):
    return (grad_unit - unit * jnp.sum(unit * grad_unit, axis=1, keepdims=True)) / length


def dot_nn(a, b):
    return lax.dot_general(a, b, (((1,), (0,)), ((), ())), preferred_element_type=F32)


def dot_nt(a, b):
    return lax.dot_general(a, b, (((1,), (1,)), ((), ())), preferred_element_type=F32)


def dot_tn(a, b):
    return lax.dot_general(a, b, (((0,), (0,)), ((), ())), preferred_element_type=F32)


def tile(index, size):
    return pl.ds(pl.multiple_of(index * size, size), size)


def make_kernel(n_sec, n_dp, n_mp):
    cores = 2 if n_mp % 2 == 0 else 1
    chips = n_mp // cores

    def kernel(
        text, image, scale_ref, hidden, w_in, w_out,
        image_out, input_out, first_out, second_out,
        text_low, cols, scores, sgrad, row_max, row_lse, row_st, row_rx, col_st, col_rx,
        wi_all, wo_all, t_tx, t_rx, t_own, g_all, g_acc, g_new, act_all, pre_all,
        w_tx, w_rx, i_tx, i_rx,
        gat_s, gat_r, fwd_s, fwd_r, cs_s, cs_r, rs_s, rs_r, wi_s, wi_r, wo_s, wo_r,
        t_s, t_r, g_s, g_r, x_s, x_r, in_s, in_r, ix_s, ix_r, w_s, w_r, im_s, im_r, io_s, io_r,
    ):
        s = lax.axis_index("section")
        d = lax.axis_index("dp")
        m = lax.axis_index("mp")
        last = n_sec - 1
        rows = text.shape[0]
        own = image.shape[0]
        half = own // n_sec
        quarter = rows // n_mp
        step = quarter // PIECES
        feats = text.shape[1]
        share = feats // n_dp
        width = feats // n_sec
        mult = scale_ref[0]
        core = lax.rem(m, cores)
        chip = m // cores

        def copy(src, dst, send, recv, where):
            return pltpu.make_async_remote_copy(
                src_ref=src, dst_ref=dst, send_sem=send, recv_sem=recv,
                device_id=where, device_id_type=MESH,
            )

        def others(mine, count):
            return [lax.rem(mine + k, count) for k in range(1, count)]

        def sources(mine, count):
            return [lax.rem(mine + count - k, count) for k in range(1, count)]

        barrier = pltpu.get_barrier_semaphore()
        for p in others(d, n_dp):
            pl.semaphore_signal(barrier, inc=1, device_id={"dp": p}, device_id_type=MESH)
        for p in others(m, n_mp):
            pl.semaphore_signal(barrier, inc=1, device_id={"mp": p}, device_id_type=MESH)
        for p in others(s, n_sec):
            pl.semaphore_signal(barrier, inc=1, device_id={"section": p}, device_id_type=MESH)

        own_unit, _ = unit_rows(image[...])
        cols[tile(d, own), :] = own_unit.astype(BF16)
        pl.semaphore_wait(barrier, n_dp + n_mp + n_sec - 3)

        def cut(block, sec):
            return cols.at[pl.ds(pl.multiple_of(block * own + sec * half, half), half), :]

        gathers = []
        for p in others(d, n_dp):
            c = copy(cut(d, s), cut(d, s), gat_s.at[p], gat_r.at[d], {"dp": p})
            c.start()
            gathers.append(c)

        class Spread:
            def __init__(self, slot, send, recv):
                self.slot, self.send, self.recv = slot, send, recv
                self.sent = []

            def push(self, index, to):
                c = copy(self.slot(index), self.slot(index), self.send(len(self.sent)),
                         self.recv(index), {"mp": to})
                c.start()
                self.sent.append(c)

            def arrived(self, index):
                copy(self.slot(index), self.slot(index), self.send(0),
                     self.recv(index), {"mp": lax.rem(m + 1, n_mp)}).wait_recv()

            def start(self):
                for q in others(chip, chips):
                    self.push(m, q * cores + core)
                for e in others(core, cores):
                    self.push(m, chip * cores + e)

            def relay(self):
                for q in sources(chip, chips):
                    index = q * cores + core
                    self.arrived(index)
                    for e in others(core, cores):
                        self.push(index, chip * cores + e)

            def finish(self):
                for e in sources(core, cores):
                    self.arrived(chip * cores + e)
                    for q in sources(chip, chips):
                        self.arrived(q * cores + e)

            def drain(self):
                for c in self.sent:
                    c.wait_send()

        wi_all[m] = w_in[...]
        wo_all[m] = w_out[...]
        wi_spread = Spread(lambda k: wi_all.at[k], lambda k: wi_s.at[k], lambda k: wi_r.at[k])
        wo_spread = Spread(lambda k: wo_all.at[k], lambda k: wo_s.at[k], lambda k: wo_r.at[k])
        wi_spread.start()
        wo_spread.start()

        @pl.loop(0, n_mp)
        def _(r):
            unit, _ = unit_rows(text[tile(r, quarter), :])
            text_low[tile(r, quarter), :] = unit.astype(BF16)

        row_max[...] = jnp.full(row_max.shape, -1e30, F32)

        def block_scores(p):
            piece = cols[tile(p, own), :]

            def chunk(r, peak):
                value = mult * dot_nt(text_low[tile(r, quarter), :], piece)
                scores[tile(r, quarter), tile(p, own)] = value
                best = row_max[tile(r, quarter), :]
                for k in range(0, own, LANES):
                    best = jnp.maximum(best, value[:, k : k + LANES])
                row_max[tile(r, quarter), :] = best
                return jnp.maximum(peak, jnp.max(value, axis=0, keepdims=True))

            peak = lax.fori_loop(0, n_mp, chunk, jnp.full((1, own), -1e30, F32))

            def total(r, acc):
                value = scores[tile(r, quarter), tile(p, own)]
                return acc + jnp.sum(jnp.exp(value - peak), axis=0, keepdims=True)

            acc = lax.fori_loop(0, n_mp, total, jnp.zeros((1, own), F32))
            col_st[pl.ds(p, 1), :] = peak
            col_st[pl.ds(n_dp + p, 1), :] = acc

        block_scores(d)
        forwards = []
        for k, p in enumerate(sources(d, n_dp)):
            copy(cut(p, s), cut(p, s), gat_s.at[p], gat_r.at[p], {"dp": p}).wait_recv()
            for t in others(s, n_sec):
                c = copy(cut(p, s), cut(p, s), fwd_s.at[t, p], fwd_r.at[s, p], {"section": t})
                c.start()
                forwards.append(c)
        for p in sources(d, n_dp):
            for t in sources(s, n_sec):
                copy(cut(p, t), cut(p, t), fwd_s.at[t, p], fwd_r.at[t, p],
                     {"section": t}).wait_recv()
            block_scores(p)

        col_rx[d] = col_st[...]
        col_sent = []
        for p in others(d, n_dp):
            c = copy(col_st, col_rx.at[d], cs_s.at[p], cs_r.at[d], {"dp": p})
            c.start()
            col_sent.append(c)

        for r in range(n_mp):
            part = pl.ds(r * quarter, quarter)
            peak = jnp.max(row_max[part, :], axis=1, keepdims=True)

            def total(p, acc):
                value = jnp.exp(scores[part, tile(p, own)] - peak)
                for k in range(0, own, LANES):
                    acc = acc + value[:, k : k + LANES]
                return acc

            acc = lax.fori_loop(0, n_dp, total, jnp.zeros((quarter, LANES), F32))
            acc = jnp.sum(acc, axis=1, keepdims=True)
            wide_peak = jnp.broadcast_to(peak, (quarter, LANES)).T
            wide_sum = jnp.broadcast_to(acc, (quarter, LANES)).T
            row_st[r : r + 1, :] = wide_peak[0:1, :]
            row_st[n_mp + r : n_mp + r + 1, :] = wide_sum[0:1, :]

        row_rx[m] = row_st[...]
        row_sent = []
        for p in others(m, n_mp):
            c = copy(row_st, row_rx.at[m], rs_s.at[p], rs_r.at[m], {"mp": p})
            c.start()
            row_sent.append(c)

        def merge(rx, count, n):
            peak = rx[0, 0:n, :]
            for k in range(1, count):
                peak = jnp.maximum(peak, rx[k, 0:n, :])
            acc = jnp.zeros(peak.shape, F32)
            for k in range(count):
                acc = acc + rx[k, n : 2 * n, :] * jnp.exp(rx[k, 0:n, :] - peak)
            return peak + jnp.log(acc)

        for p in sources(d, n_dp):
            copy(col_st, col_rx.at[p], cs_s.at[p], cs_r.at[p], {"dp": p}).wait_recv()
        col_lse = merge(col_rx, n_dp, n_dp)
        col_st_rows = [col_lse[k : k + 1, :] for k in range(n_dp)]
        for p in sources(m, n_mp):
            copy(row_st, row_rx.at[p], rs_s.at[p], rs_r.at[p], {"mp": p}).wait_recv()
        merged = merge(row_rx, n_mp, n_mp)
        for r in range(n_mp):
            row_lse[r] = jnp.broadcast_to(merged[r : r + 1, :], (LANES, quarter)).T

        def score_rows(r):
            line = row_lse[r]
            text_id = lax.broadcasted_iota(jnp.int32, (quarter, LANES), 0) + d * rows + r * quarter
            for p in range(n_dp):
                for k in range(0, own, LANES):
                    value = scores[tile(r, quarter), p * own + k : p * own + k + LANES]
                    both = jnp.exp(value - line) + jnp.exp(value - col_st_rows[p][:, k : k + LANES])
                    image_id = lax.broadcasted_iota(jnp.int32, (quarter, LANES), 1) + (
                        (p * n_mp + m) * own + k
                    )
                    out = 0.5 * both - jnp.where(text_id == image_id, 1.0, 0.0)
                    sgrad[tile(r, quarter), p * own + k : p * own + k + LANES] = out.astype(BF16)

        @pl.loop(0, n_mp)
        def _(k):
            to_chip = lax.rem(chip + 1 + k // cores, chips)
            r = to_chip * cores + lax.rem(core + 1 + lax.rem(k, cores), cores)
            score_rows(r)

            @pl.when(s == last)
            def _():
                value = dot_nn(sgrad[tile(r, quarter), :], cols[...])

                @pl.when(k < n_mp - 1)
                def _():
                    t_tx[r] = value.astype(BF16)
                    copy(t_tx.at[r], t_rx.at[m], t_s.at[r], t_r.at[m], {"mp": r}).start()

                @pl.when(k == n_mp - 1)
                def _():
                    t_own[...] = value

        def image_part(p):
            at = pl.ds(pl.multiple_of(p * own + s * half, half), half)
            return dot_tn(sgrad[:, at], text_low[...])

        image_sent = []
        for p in others(d, n_dp):
            i_tx[p] = image_part(p).astype(BF16)
            c = copy(i_tx.at[p], i_rx.at[d], im_s.at[p], im_r.at[d], {"dp": p})
            c.start()
            image_sent.append(c)

        wi_spread.relay()
        wo_spread.relay()

        mine = tile(m, quarter)

        @pl.when(s == last)
        def _():
            total = t_own[...]
            for p in sources(m, n_mp):
                copy(t_tx.at[p], t_rx.at[p], t_s.at[p], t_r.at[p], {"mp": p}).wait_recv()
                total = total + t_rx[p].astype(F32)
            unit, length = unit_rows(text[mine, :])
            g_all[m] = unit_backward(unit, length, mult * total).astype(BF16)

        wi_spread.finish()
        wo_spread.finish()

        def slopes(pre, back):
            sigm = 1.0 / (1.0 + jnp.exp(-GELU * pre))
            grad = back * (sigm + GELU * pre * sigm * (1.0 - sigm))
            return (pre * sigm).astype(BF16), grad.astype(BF16)

        def slab(k):
            return input_out.at[tile(k, quarter), :]

        def final(t, piece):
            part = pl.ds(piece * step, step)
            return copy(g_new.at[part, t * width : (t + 1) * width], slab(m).at[part, :],
                        ix_s.at[t, piece], ix_r.at[piece], {"section": t})

        def hop(piece, to):
            part = pl.ds(piece * step, step)
            return copy(g_new.at[part, :], g_all.at[m, part, :], x_s.at[piece], x_r.at[piece],
                        {"section": to})

        g_spreads = []
        for piece in range(PIECES):
            part = pl.ds(piece * step, step)

            @pl.when(s != last)
            def _():
                hop(piece, s + 1).wait_recv()

            spread = Spread(lambda k, part=part: g_all.at[k, part, :],
                            lambda k, piece=piece: g_s.at[piece, k],
                            lambda k, piece=piece: g_r.at[piece, k])
            spread.start()
            g_spreads.append(spread)

        g_acc[...] = g_all[m].astype(F32)

        @pl.loop(0, n_mp)
        def _(j):
            pre = dot_nn(hidden[mine, :], wi_all[j])
            back = dot_nt(g_all[m], wo_all[j])
            _, grad = slopes(pre, back)
            g_acc[...] += dot_nt(grad, wi_all[j])

        g_new[...] = g_acc[...].astype(BF16)

        for piece in range(PIECES):

            @pl.when(s > 0)
            def _():
                hop(piece, s - 1).start()

            @pl.when(s == 0)
            def _():
                for t in range(1, n_sec):
                    final(t, piece).start()

        @pl.when(s == 0)
        def _():
            input_out[mine, :] = g_new[:, 0:width]

        for spread in g_spreads:
            spread.relay()
        in_spread = Spread(slab, lambda k: in_s.at[k], lambda k: in_r.at[k])

        def weight_rows(r):
            pre = dot_nn(hidden[tile(r, quarter), :], w_in[...])
            back = dot_nt(g_all[r], w_out[...])
            act, grad = slopes(pre, back)
            act_all[tile(r, quarter), :] = act
            pre_all[tile(r, quarter), :] = grad

        weight_rows(m)
        for q in sources(chip, chips):
            weight_rows(q * cores + core)
        for e in sources(core, cores):
            for index in [chip * cores + e] + [q * cores + e for q in sources(chip, chips)]:
                for spread in g_spreads:
                    spread.arrived(index)
                weight_rows(index)

        g_rows = g_all[...].reshape(rows, feats)
        grad_second = dot_tn(g_rows, act_all[...])
        for p in range(n_dp):
            w_tx[p, 1] = grad_second[p * share : (p + 1) * share, :].astype(BF16)
        weight_sent = []

        def send_weights(which):
            for p in others(d, n_dp):
                c = copy(w_tx.at[p, which], w_rx.at[d, which], w_s.at[which, p],
                         w_r.at[which, d], {"dp": p})
                c.start()
                weight_sent.append(c)

        send_weights(1)
        grad_first = dot_tn(hidden[...], pre_all[...])
        for p in range(n_dp):
            w_tx[p, 0] = grad_first[p * share : (p + 1) * share, :].astype(BF16)
        send_weights(0)

        @pl.when(s != 0)
        def _():
            for piece in range(PIECES):
                final(0, piece).wait_recv()

        in_spread.start()

        image_half = pl.ds(pl.multiple_of(s * half, half), half)
        total = image_part(d)
        for p in sources(d, n_dp):
            copy(i_tx.at[p], i_rx.at[p], im_s.at[p], im_r.at[p], {"dp": p}).wait_recv()
            total = total + i_rx[p].astype(F32)
        unit, length = unit_rows(image[image_half, :])
        image_out[image_half, :] = unit_backward(unit, length, mult * total).astype(BF16)
        out_sent = []
        for t in others(s, n_sec):
            c = copy(image_out.at[image_half, :], image_out.at[image_half, :],
                     io_s.at[t], io_r.at[s], {"section": t})
            c.start()
            out_sent.append(c)

        in_spread.relay()
        in_spread.finish()

        for which, out in ((1, second_out), (0, first_out)):
            total = w_tx[d, which].astype(F32)
            for p in sources(d, n_dp):
                copy(w_tx.at[p, which], w_rx.at[p, which], w_s.at[which, p],
                     w_r.at[which, p], {"dp": p}).wait_recv()
                total = total + w_rx[p, which].astype(F32)
            out[...] = total

        for t in sources(s, n_sec):
            part = image_out.at[pl.ds(pl.multiple_of(t * half, half), half), :]
            copy(part, part, io_s.at[t], io_r.at[t], {"section": t}).wait_recv()

        for c in gathers + forwards + col_sent + row_sent + image_sent + weight_sent + out_sent:
            c.wait_send()
        for spread in (wi_spread, wo_spread, *g_spreads, in_spread):
            spread.drain()

        @pl.when(s == last)
        def _():
            for p in others(m, n_mp):
                copy(t_tx.at[p], t_rx.at[m], t_s.at[p], t_r.at[m], {"mp": p}).wait_send()

        @pl.when(s > 0)
        def _():
            for piece in range(PIECES):
                hop(piece, s - 1).wait_send()

        @pl.when(s == 0)
        def _():
            for t in range(1, n_sec):
                for piece in range(PIECES):
                    final(t, piece).wait_send()

    return kernel


def solution(mesh):
    n_sec, n_dp, n_mp = mesh.shape["section"], mesh.shape["dp"], mesh.shape["mp"]

    def body(text, image, scale, hidden, w_in, w_out):
        rows, feats = text.shape
        own = image.shape[0]
        hid = w_in.shape[2]
        quarter, half, share = rows // n_mp, own // n_sec, feats // n_dp
        columns = own * n_dp
        dma = pltpu.SemaphoreType.DMA
        vmem = pl.BlockSpec(memory_space=pltpu.VMEM)
        out = pl.pallas_call(
            make_kernel(n_sec, n_dp, n_mp),
            out_shape=(
                jax.ShapeDtypeStruct((own, feats), BF16),
                jax.ShapeDtypeStruct((rows, feats // n_sec), BF16),
                jax.ShapeDtypeStruct((share, hid), F32),
                jax.ShapeDtypeStruct((share, hid), F32),
            ),
            in_specs=[vmem, vmem, pl.BlockSpec(memory_space=pltpu.SMEM), vmem, vmem, vmem],
            out_specs=(vmem,) * 4,
            scratch_shapes=[
                pltpu.VMEM((rows, feats), BF16),
                pltpu.VMEM((columns, feats), BF16),
                pltpu.VMEM((rows, columns), F32),
                pltpu.VMEM((rows, columns), BF16),
                pltpu.VMEM((rows, LANES), F32),
                pltpu.VMEM((n_mp, quarter, LANES), F32),
                pltpu.VMEM((2 * n_mp, quarter), F32),
                pltpu.VMEM((n_mp, 2 * n_mp, quarter), F32),
                pltpu.VMEM((2 * n_dp, own), F32),
                pltpu.VMEM((n_dp, 2 * n_dp, own), F32),
                pltpu.VMEM((n_mp, feats, hid), BF16),
                pltpu.VMEM((n_mp, hid, feats), BF16),
                pltpu.VMEM((n_mp, quarter, feats), BF16),
                pltpu.VMEM((n_mp, quarter, feats), BF16),
                pltpu.VMEM((quarter, feats), F32),
                pltpu.VMEM((n_mp, quarter, feats), BF16),
                pltpu.VMEM((quarter, feats), F32),
                pltpu.VMEM((quarter, feats), BF16),
                pltpu.VMEM((rows, hid), BF16),
                pltpu.VMEM((rows, hid), BF16),
                pltpu.VMEM((n_dp, 2, share, hid), BF16),
                pltpu.VMEM((n_dp, 2, share, hid), BF16),
                pltpu.VMEM((n_dp, half, feats), BF16),
                pltpu.VMEM((n_dp, half, feats), BF16),
                dma((n_dp,)), dma((n_dp,)),
                dma((n_sec, n_dp)), dma((n_sec, n_dp)),
                dma((n_dp,)), dma((n_dp,)),
                dma((n_mp,)), dma((n_mp,)),
                dma((2 * n_mp,)), dma((n_mp,)),
                dma((2 * n_mp,)), dma((n_mp,)),
                dma((n_mp,)), dma((n_mp,)),
                dma((PIECES, 2 * n_mp)), dma((PIECES, n_mp)),
                dma((PIECES,)), dma((PIECES,)),
                dma((2 * n_mp,)), dma((n_mp,)),
                dma((n_sec, PIECES)), dma((PIECES,)),
                dma((2, n_dp)), dma((2, n_dp)),
                dma((n_dp,)), dma((n_dp,)),
                dma((n_sec,)), dma((n_sec,)),
            ],
            compiler_params=pltpu.CompilerParams(
                collective_id=0, has_side_effects=True, vmem_limit_bytes=63000000
            ),
        )(text, image, scale, hidden[0], w_in[0], w_out[0])
        image_grad, input_grad, first, second = out
        return (image_grad, input_grad, first[None], second[None])

    return jax.shard_map(
        body,
        mesh=mesh,
        in_specs=(
            P("dp", None),
            P(("dp", "mp"), None),
            P(),
            P("section", "dp", None),
            P("section", None, "mp"),
            P("section", "mp", None),
        ),
        out_specs=(
            P(("dp", "mp"), None),
            P("dp", "section"),
            P("section", "dp", "mp"),
            P("section", "dp", "mp"),
        ),
        check_vma=False,
    )
```

profile of v0, /device:TPU:0, one launch (start us, length us, event | category | flops | bytes accessed | tf_op | source)
XLA Modules:
  0.0 147.8 jit_solution(5517499417285378321)
XLA Ops:
  1.3 142.4 %shard_map.93 = (bf16[256,512]{1,0:T(8,128)(2,1)}, bf16[1024,256]{1,0:T(8,128)(2,1)}, f32[32,512]{1,0:T(8,128)}, f32[32,512]{1,0:T(8,128)}) custom-call(bf16[1024,512]{1,0:T(8,128)(2,1)} %text.1, bf16[256,512]{1,0:T(8,128)(2,1)} %image.1, f32[1]{0:T(128)S(6)} %copy.14.scale_ref, bf16[1024,512]{1,0:T(8,128)(2,1)} %bitcast.5, bf16[512,512]{1,0:T(8,128)(2,1)} %bitcast.6, ...), custom_call_target="tpu_custom_call" | custom-call | tf_op jit(solution)/shard_map/pallas_call | solution.py:470
  143.7 0.0 copy-start
  143.7 1.7 %copy.15 = bf16[256,512]{1,0:T(8,128)(2,1)} copy(bf16[256,512]{1,0:T(8,128)(2,1)} %get-tuple-element.16) | data formatting | bytes 524288
  145.4 0.0 copy-done
  145.4 0.0 copy-start.2
  145.5 0.8 copy.16
  146.2 0.1 copy-done.2
  146.3 0.0 copy-start.1
  146.3 0.6 copy.17
  146.9 0.2 copy-done.1
  147.2 0.6 copy.18
Async XLA Ops:
  143.7 1.7 %copy-start = (bf16[1024,256]{1,0:T(8,128)(2,1)S(1)}, bf16[1024,256]{1,0:T(8,128)(2,1)}, u32[]{:S(2)}) copy-start(bf16[1024,256]{1,0:T(8,128)(2,1)} %get-tuple-element.17) | copy-start | bytes 1572868
  145.4 0.9 copy-start.2
  146.3 0.9 copy-start.1
where the time goes:
time: 149 us; the launch traced here: 148 us
  Pallas kernels  142 us (95%)
  local copies, waits for them, and re-layouts  4.08 us (3%)
    pallas_call x1, Pallas kernels, body(): pl.pallas_call(make_kernel(n_sec, n_dp, n_mp), out_shape=(jax.ShapeDtypeS...  142 us
    unnamed x10, local copies, waits for them, and re-layouts  4.08 us

commit v1 on v0

v1 whole, which is shorter than its diff:
```python
import jax
import jax.numpy as jnp
from jax import lax
from jax.experimental import pallas as pl
from jax.experimental.pallas import tpu as pltpu
from jax.sharding import PartitionSpec as P

MESH = pl.DeviceIdType.MESH
F32 = jnp.float32
BF16 = jnp.bfloat16
GELU = 1.702
LOG2E = 1.4426950408889634
LANES = 128
CORES = 2


def unit_rows(values):
    wide = values.astype(F32)
    length = jnp.sqrt(jnp.sum(wide * wide, axis=1, keepdims=True) + 1.0)
    return (wide / length, length)


def unit_backward(unit, length, grad_unit):
    return (grad_unit - unit * jnp.sum(unit * grad_unit, axis=1, keepdims=True)) / length


def dot_nn(a, b):
    return lax.dot_general(a, b, (((1,), (0,)), ((), ())), preferred_element_type=F32)


def dot_nt(a, b):
    return lax.dot_general(a, b, (((1,), (1,)), ((), ())), preferred_element_type=F32)


def dot_tn(a, b):
    return lax.dot_general(a, b, (((0,), (0,)), ((), ())), preferred_element_type=F32)


def tile(index, size):
    return pl.ds(pl.multiple_of(index * size, size), size)


def make_kernel(n_sec, n_dp, n_mp):
    chips = n_mp // CORES
    line = n_sec * chips
    n_el = n_sec * n_mp

    def kernel(
        text, image, scale_ref, hidden, w_in, w_out,
        image_out, input_out, first_out, second_out,
        text_low, cols, scores, sgrad, row_max, row_lse, col_lse, row_st, row_rx, col_st, col_rx,
        wi_all, wo_all, h_own, t_full, t_keep, t_sx, t_sr, t_tx, t_rx,
        g_st, g_all, g_acc, in_st, act_all, slope_all, pre_all,
        w_tx, w_rx, i_tx, i_rx,
        gat_s, gat_r, cs_s, cs_r, rs_s, rs_r, ww_s, ww_r, h_s, h_r,
        ts_s, ts_r, tc_s, tc_r, gs_s, gs_r, gr_s, in_s, in_r, ir_s,
        w_s, w_r, im_s, im_r, io_s, io_r,
    ):
        s = lax.axis_index("section")
        d = lax.axis_index("dp")
        m = lax.axis_index("mp")
        rows, feats = text.shape
        own = image.shape[0]
        half = own // n_sec
        chunk = rows // n_el
        pair = rows // line
        share = feats // n_dp
        width = feats // n_sec
        mult = scale_ref[0]
        mult2 = mult * LOG2E
        core = lax.rem(m, CORES)
        sib = 1 - core
        spot = s * chips + m // CORES
        e = s * n_mp + m

        def at(place, who):
            return {"section": place // chips, "mp": lax.rem(place, chips) * CORES + who}

        def far(step):
            return lax.rem(spot + step, line)

        def copy(src, dst, send, recv, where):
            return pltpu.make_async_remote_copy(
                src_ref=src, dst_ref=dst, send_sem=send, recv_sem=recv,
                device_id=where, device_id_type=MESH,
            )

        def arrived(ref, recv):
            copy(ref, ref, h_s, recv, at(spot, sib)).wait_recv()

        def others(mine, count):
            return [lax.rem(mine + k, count) for k in range(1, count)]

        def sources(mine, count):
            return [lax.rem(mine + count - k, count) for k in range(1, count)]

        sent = []

        def push(*args):
            c = copy(*args)
            c.start()
            sent.append(c)

        with jax.named_scope("a_barrier"):
            barrier = pltpu.get_barrier_semaphore()
            for p in others(d, n_dp):
                pl.semaphore_signal(barrier, inc=1, device_id={"dp": p}, device_id_type=MESH)
            for q in others(e, n_el):
                pl.semaphore_signal(
                    barrier, inc=1, device_id={"section": q // n_mp, "mp": lax.rem(q, n_mp)},
                    device_id_type=MESH,
                )
            own_unit, _ = unit_rows(image[tile(s, half), :])
            cols[tile(d, half), :] = own_unit.astype(BF16)
            h_own[s] = hidden[tile(e, chunk), :]
            wi_all[e] = w_in[...]
            wo_all[e] = w_out[...]
            pl.semaphore_wait(barrier, n_dp + n_el - 2)

        for p in others(d, n_dp):
            push(cols.at[tile(d, half), :], cols.at[tile(d, half), :], gat_s.at[p], gat_r.at[d],
                 {"dp": p})

        mate = (1 - s) * n_mp + m
        push(hidden.at[tile(mate, chunk), :], h_own.at[s], h_s, h_r, {"section": 1 - s})
        ww = ((w_in, wi_all), (w_out, wo_all))
        for which in (0, 1):
            push(ww[which][0], ww[which][1].at[e], ww_s.at[which, 1], ww_r.at[which, e],
                 at(far(line - 1), core))
            push(ww[1 - which][0], ww[1 - which][1].at[e], ww_s.at[1 - which, 2],
                 ww_r.at[1 - which, e], at(far(1), core))
        for which in (0, 1):
            push(ww[which][0], ww[which][1].at[e], ww_s.at[which, 0], ww_r.at[which, e],
                 at(spot, sib))

        def relay_weight(which, step, slot, onward=None):
            index = far(step) * CORES + core
            buf = ww[which][1].at[index]
            arrived(buf, ww_r.at[which, index])
            if onward is not None:
                push(buf, buf, ww_s.at[which, 3], ww_r.at[which, index], at(far(onward), core))
            push(buf, buf, ww_s.at[which, slot], ww_r.at[which, index], at(spot, sib))

        def sigmoid(pre):
            return 1.0 / (1.0 + jnp.exp(-GELU * pre))

        with jax.named_scope("b_pre"):
            @pl.loop(0, line)
            def _(r):
                unit, _ = unit_rows(text[tile(r, pair), :])
                text_low[tile(r, pair), :] = unit.astype(BF16)

            @pl.loop(0, line)
            def _(r):
                pre = dot_nn(hidden[tile(r, pair), :], w_in[...])
                sigm = sigmoid(pre)
                act_all[tile(r, pair), :] = (pre * sigm).astype(BF16)
                slope_all[tile(r, pair), :] = sigm + GELU * pre * sigm * (1.0 - sigm)

        row_max[...] = jnp.full(row_max.shape, -1e30, F32)

        def block_scores(p):
            piece = cols[tile(p, half), :]

            def part(r, peak):
                value = mult2 * dot_nt(text_low[tile(r, pair), :], piece)
                scores[p, tile(r, pair), :] = value
                row_max[tile(r, pair), :] = jnp.maximum(row_max[tile(r, pair), :], value)
                return jnp.maximum(peak, jnp.max(value, axis=0, keepdims=True))

            peak = lax.fori_loop(0, line, part, jnp.full((1, half), -1e30, F32))

            def total(r, acc):
                value = scores[p, tile(r, pair), :]
                return acc + jnp.sum(jnp.exp2(value - peak), axis=0, keepdims=True)

            acc = lax.fori_loop(0, line, total, jnp.zeros((1, half), F32))
            col_st[pl.ds(p, 1), :] = peak
            col_st[pl.ds(n_dp + p, 1), :] = acc

        with jax.named_scope("c_blocks"):
            block_scores(d)
            for k, p in enumerate(sources(d, n_dp)):
                arrived(cols.at[tile(p, half), :], gat_r.at[p])
                block_scores(p)
                if k == n_dp // 2:
                    relay_weight(0, 1, 4, line - 1)
                    relay_weight(1, line - 1, 4, 1)

        with jax.named_scope("d_colsend"):
            col_rx[d] = col_st[...]
            for p in others(d, n_dp):
                push(col_st, col_rx.at[d], cs_s.at[p], cs_r.at[d], {"dp": p})

        with jax.named_scope("e_rowstat"):
            for r in range(n_el):
                part = pl.ds(r * chunk, chunk)
                peak = jnp.max(row_max[part, :], axis=1, keepdims=True)

                def total(p, acc):
                    return acc + jnp.exp2(scores[p, part, :] - peak)

                acc = lax.fori_loop(0, n_dp, total, jnp.zeros((chunk, LANES), F32))
                acc = jnp.sum(acc, axis=1, keepdims=True)
                row_st[r : r + 1, :] = jnp.broadcast_to(peak, (chunk, LANES)).T[0:1, :]
                row_st[n_el + r : n_el + r + 1, :] = jnp.broadcast_to(acc, (chunk, LANES)).T[0:1, :]
            row_rx[e] = row_st[...]
            for q in others(e, n_el):
                push(row_st, row_rx.at[e], rs_s.at[q], rs_r.at[e],
                     {"section": q // n_mp, "mp": lax.rem(q, n_mp)})

        def merge(rx, count, n):
            peak = rx[0, 0:n, :]
            for k in range(1, count):
                peak = jnp.maximum(peak, rx[k, 0:n, :])
            acc = jnp.zeros(peak.shape, F32)
            for k in range(count):
                acc = acc + rx[k, n : 2 * n, :] * jnp.exp2(rx[k, 0:n, :] - peak)
            return peak + (jnp.log(acc) * LOG2E + 1.0)

        with jax.named_scope("f_relay"):
            relay_weight(1, 1, 5)
            relay_weight(0, line - 1, 5)

        with jax.named_scope("f_merge"):
            for p in sources(d, n_dp):
                arrived(col_rx.at[p], cs_r.at[p])
            col_lse[...] = merge(col_rx, n_dp, n_dp)
            for q in sources(e, n_el):
                arrived(row_rx.at[q], rs_r.at[q])
            merged = merge(row_rx, n_el, n_el)
            for r in range(n_el):
                row_lse[r * chunk : (r + 1) * chunk, :] = jnp.broadcast_to(
                    merged[r : r + 1, :], (LANES, chunk)).T

        def score_rows(r):
            base = row_lse[tile(r, pair), :]
            for p in range(n_dp):
                value = scores[p, tile(r, pair), :]
                both = jnp.exp2(value - base) + jnp.exp2(value - col_lse[p : p + 1, :])
                sgrad[tile(r, pair), p * half : (p + 1) * half] = both.astype(BF16)

            @pl.when(r == m)
            def _():
                line_at = tile(m * n_sec + s, half)
                value = scores[d, line_at, :]
                both = jnp.exp2(value - row_lse[line_at, :]) + jnp.exp2(
                    value - col_lse[pl.ds(d, 1), :])
                diagonal = lax.broadcasted_iota(jnp.int32, (half, half), 0) == (
                    lax.broadcasted_iota(jnp.int32, (half, half), 1))
                sgrad[line_at, tile(d, half)] = (
                    both - jnp.where(diagonal, 1.0, 0.0)).astype(BF16)

        def join(where):
            arrived(t_sr.at[where], ts_r.at[where])
            return t_keep[where] + t_sr[where].astype(F32)

        hops = (2, 3, 1, 0) if line == 4 else tuple(range(line - 1, -1, -1))

        def t_send(where, slot):
            return copy(t_tx.at[where], t_rx.at[spot], tc_s.at[slot], tc_r.at[spot],
                        at(where, core))

        with jax.named_scope("g_scorerows"):
            for i, hop in enumerate(hops):
                where = far(hop)
                score_rows(where)
                t_full[...] = dot_nn(sgrad[tile(where, pair), :], cols[...])
                t_sx[where] = t_full[tile(sib, chunk), :].astype(BF16)
                push(t_sx.at[where], t_sr.at[where], ts_s.at[i], ts_r.at[where], at(spot, sib))
                t_keep[where] = t_full[tile(core, chunk), :]
                if i > 0:
                    last = far(hops[i - 1])
                    t_tx[last] = join(last).astype(BF16)
                    push(t_tx.at[last], t_rx.at[spot], tc_s.at[i], tc_r.at[spot],
                         at(last, core))

        def image_part(p):
            return dot_tn(sgrad[:, tile(p, half)], text_low[...])

        with jax.named_scope("h_image"):
            for p in others(d, n_dp):
                i_tx[p] = image_part(p).astype(BF16)
                push(i_tx.at[p], i_rx.at[d], im_s.at[p], im_r.at[d], {"dp": p})

        mine = tile(e, chunk)

        with jax.named_scope("i_topgrad"):
            total = join(spot)
            for hop in hops[:-1]:
                where = far(hop)
                arrived(t_rx.at[where], tc_r.at[where])
                total = total + t_rx[where].astype(F32)
            unit, length = unit_rows(text[mine, :])
            g_st[n_sec - 1] = unit_backward(unit, length, mult * total).astype(BF16)

        with jax.named_scope("j_weights"):
            arrived(h_own.at[1 - s], h_r)
            relay_weight(0, 2, 6)
            relay_weight(1, 2, 6)
            for step in range(line):
                index = far(step) * CORES + sib
                for which in (0, 1):
                    arrived(ww[which][1].at[index], ww_r.at[which, index])

        def spread(layer):
            for c in range(chips):
                place = layer * chips + c

                @pl.when(spot != place)
                def _():
                    copy(g_st.at[layer], g_all.at[e], gs_s.at[layer, c], gs_r.at[e],
                         at(place, core)).start()

            @pl.when(s == layer)
            def _():
                g_all[e] = g_st[layer]
                copy(g_st.at[layer], g_all.at[e], gs_s.at[layer, chips], gs_r.at[e],
                     at(spot, sib)).start()

        def drain_spread(layer):
            for c in range(chips):
                place = layer * chips + c

                @pl.when(spot != place)
                def _():
                    copy(g_st.at[layer], g_all.at[e], gs_s.at[layer, c], gs_r.at[e],
                         at(place, core)).wait_send()

            @pl.when(s == layer)
            def _():
                copy(g_st.at[layer], g_all.at[e], gs_s.at[layer, chips], gs_r.at[e],
                     at(spot, sib)).wait_send()

        def feed_forward(layer):
            spread(layer)
            g_acc[...] = g_st[layer].astype(F32)

            @pl.loop(0, n_mp)
            def _(j):
                index = layer * n_mp + j
                pre = dot_nn(h_own[layer], wi_all[index])
                back = dot_nt(g_st[layer], wo_all[index])
                sigm = sigmoid(pre)
                grad = (back * (sigm + GELU * pre * sigm * (1.0 - sigm))).astype(BF16)
                g_acc[...] += dot_nt(grad, wi_all[index])

            if layer > 0:
                g_st[layer - 1] = g_acc[...].astype(BF16)

        def slab(k):
            return input_out.at[tile(k, chunk), :]

        with jax.named_scope("k_ffn"):
            for layer in range(n_sec - 1, -1, -1):
                feed_forward(layer)

        with jax.named_scope("l_inspread"):
            for t in range(n_sec):
                in_st[t] = g_acc[:, t * width : (t + 1) * width].astype(BF16)
            input_out[mine, :] = in_st[s]
            push(in_st.at[s], slab(e), in_s.at[0], in_r.at[e], at(spot, sib))
            for hop in hops[:-1]:
                where = far(hop)
                push(in_st.at[where // chips], slab(e), in_s.at[hop], in_r.at[e],
                     at(where, core))

        def weight_rows(k):
            back = dot_nt(g_all[k], w_out[...])
            pre_all[tile(k, chunk), :] = (back * slope_all[tile(k, chunk), :]).astype(BF16)

        with jax.named_scope("m_weightrows"):
            weight_rows(e)
            for hop in (1, 3, 2) if line == 4 else range(1, line):
                index = far(hop) * CORES + core
                arrived(g_all.at[index], gs_r.at[index])
                push(g_all.at[index], g_all.at[index], gr_s.at[hop], gs_r.at[index],
                     at(spot, sib))
                weight_rows(index)
            for hop in (0, 1, 3, 2) if line == 4 else range(line):
                index = far(hop) * CORES + sib
                arrived(g_all.at[index], gs_r.at[index])
                weight_rows(index)

        def send_weights(which):
            for p in others(d, n_dp):
                push(w_tx.at[p, which], w_rx.at[d, which], w_s.at[which, p], w_r.at[which, d],
                     {"dp": p})

        with jax.named_scope("n_wgrad"):
            g_rows = g_all[...].reshape(rows, feats)
            grad_second = dot_tn(g_rows, act_all[...])
            for p in range(n_dp):
                w_tx[p, 1] = grad_second[p * share : (p + 1) * share, :].astype(BF16)
            send_weights(1)
            grad_first = dot_tn(hidden[...], pre_all[...])
            for p in range(n_dp):
                w_tx[p, 0] = grad_first[p * share : (p + 1) * share, :].astype(BF16)
            send_weights(0)

        with jax.named_scope("o_inrelay"):
            for hop in hops[:-1]:
                index = far(hop) * CORES + core
                arrived(slab(index), in_r.at[index])
                push(slab(index), slab(index), ir_s.at[hop], in_r.at[index], at(spot, sib))

        with jax.named_scope("p_image"):
            image_half = tile(s, half)
            total = image_part(d)
            for p in sources(d, n_dp):
                arrived(i_rx.at[p], im_r.at[p])
                total = total + i_rx[p].astype(F32)
            unit, length = unit_rows(image[image_half, :])
            image_out[image_half, :] = unit_backward(unit, length, mult * total).astype(BF16)
            push(image_out.at[image_half, :], image_out.at[image_half, :], io_s, io_r,
                 {"section": 1 - s})

        with jax.named_scope("q_wsum"):
            for which, out in ((1, second_out), (0, first_out)):
                total = w_tx[d, which].astype(F32)
                for p in sources(d, n_dp):
                    arrived(w_rx.at[p, which], w_r.at[which, p])
                    total = total + w_rx[p, which].astype(F32)
                out[...] = total

        with jax.named_scope("r_drain"):
            for step in range(line):
                index = far(step) * CORES + sib
                arrived(slab(index), in_r.at[index])
            arrived(image_out.at[tile(1 - s, half), :], io_r)
            for c in sent:
                c.wait_send()
            for layer in range(n_sec):
                drain_spread(layer)

    return kernel


def solution(mesh):
    n_sec, n_dp, n_mp = mesh.shape["section"], mesh.shape["dp"], mesh.shape["mp"]

    def body(text, image, scale, hidden, w_in, w_out):
        rows, feats = text.shape
        own = image.shape[0]
        hid = w_in.shape[2]
        half, share = own // n_sec, feats // n_dp
        columns = half * n_dp
        line = n_sec * n_mp // CORES
        n_el = n_sec * n_mp
        chunk = rows // n_el
        dma = pltpu.SemaphoreType.DMA
        vmem = pl.BlockSpec(memory_space=pltpu.VMEM)
        out = pl.pallas_call(
            make_kernel(n_sec, n_dp, n_mp),
            out_shape=(
                jax.ShapeDtypeStruct((own, feats), BF16),
                jax.ShapeDtypeStruct((rows, feats // n_sec), BF16),
                jax.ShapeDtypeStruct((share, hid), F32),
                jax.ShapeDtypeStruct((share, hid), F32),
            ),
            in_specs=[vmem, vmem, pl.BlockSpec(memory_space=pltpu.SMEM), vmem, vmem, vmem],
            out_specs=(vmem,) * 4,
            scratch_shapes=[
                pltpu.VMEM((rows, feats), BF16),
                pltpu.VMEM((columns, feats), BF16),
                pltpu.VMEM((n_dp, rows, half), F32),
                pltpu.VMEM((rows, columns), BF16),
                pltpu.VMEM((rows, LANES), F32),
                pltpu.VMEM((rows, LANES), F32),
                pltpu.VMEM((n_dp, half), F32),
                pltpu.VMEM((2 * n_el, chunk), F32),
                pltpu.VMEM((n_el, 2 * n_el, chunk), F32),
                pltpu.VMEM((2 * n_dp, half), F32),
                pltpu.VMEM((n_dp, 2 * n_dp, half), F32),
                pltpu.VMEM((n_el, feats, hid), BF16),
                pltpu.VMEM((n_el, hid, feats), BF16),
                pltpu.VMEM((n_sec, chunk, feats), BF16),
                pltpu.VMEM((CORES * chunk, feats), F32),
                pltpu.VMEM((line, chunk, feats), F32),
                pltpu.VMEM((line, chunk, feats), BF16),
                pltpu.VMEM((line, chunk, feats), BF16),
                pltpu.VMEM((line, chunk, feats), BF16),
                pltpu.VMEM((line, chunk, feats), BF16),
                pltpu.VMEM((n_sec, chunk, feats), BF16),
                pltpu.VMEM((n_el, chunk, feats), BF16),
                pltpu.VMEM((chunk, feats), F32),
                pltpu.VMEM((n_sec, chunk, feats // n_sec), BF16),
                pltpu.VMEM((rows, hid), BF16),
                pltpu.VMEM((rows, hid), F32),
                pltpu.VMEM((rows, hid), BF16),
                pltpu.VMEM((n_dp, 2, share, hid), BF16),
                pltpu.VMEM((n_dp, 2, share, hid), BF16),
                pltpu.VMEM((n_dp, half, feats), BF16),
                pltpu.VMEM((n_dp, half, feats), BF16),
                dma((n_dp,)), dma((n_dp,)),
                dma((n_dp,)), dma((n_dp,)),
                dma((n_el,)), dma((n_el,)),
                dma((2, 7)), dma((2, n_el)),
                dma, dma,
                dma((line,)), dma((line,)),
                dma((line,)), dma((line,)),
                dma((n_sec, line + 1)), dma((n_el,)),
                dma((line,)),
                dma((line,)), dma((n_el,)),
                dma((line,)),
                dma((2, n_dp)), dma((2, n_dp)),
                dma((n_dp,)), dma((n_dp,)),
                dma, dma,
            ],
            compiler_params=pltpu.CompilerParams(
                collective_id=0, has_side_effects=True, vmem_limit_bytes=63000000
            ),
        )(text, image, scale, hidden[0], w_in[0], w_out[0])
        image_grad, input_grad, first, second = out
        return (image_grad, input_grad, first[None], second[None])

    return jax.shard_map(
        body,
        mesh=mesh,
        in_specs=(
            P("dp", None),
            P(("dp", "mp"), None),
            P(),
            P("section", "dp", None),
            P("section", None, "mp"),
            P("section", "mp", None),
        ),
        out_specs=(
            P(("dp", "mp"), None),
            P("dp", "section"),
            P("section", "dp", "mp"),
            P("section", "dp", "mp"),
        ),
        check_vma=False,
    )
```

time: 149 us -> 113 us (0.76)
  Pallas kernels: 142 us -> 107 us
    pallas_call x1, Pallas kernels: 142 us -> 107 us  [body(): pl.pallas_call(make_kernel(n_sec, n_dp, n_mp), out_shape=(jax.ShapeDtypeS...]
where the time goes in v1:
time: 113 us; the launch traced here: 112 us
  Pallas kernels  107 us (95%)
  local copies, waits for them, and re-layouts  4.08 us (4%)
  between operations  1.3 us (1%)
    pallas_call x1, Pallas kernels, body(): pl.pallas_call(make_kernel(n_sec, n_dp, n_mp), out_shape=(jax.ShapeDtypeS...  107 us
    unnamed x10, local copies, waits for them, and re-layouts  4.08 us

profile of v1, /device:TPU:0, one launch (start us, length us, event | category | flops | bytes accessed | tf_op | source)
XLA Modules:
  0.0 112.4 jit_solution(124579253099002125)
XLA Ops:
  1.3 107.1 %shard_map.93 = (bf16[256,512]{1,0:T(8,128)(2,1)}, bf16[1024,256]{1,0:T(8,128)(2,1)}, f32[32,512]{1,0:T(8,128)}, f32[32,512]{1,0:T(8,128)}) custom-call(bf16[1024,512]{1,0:T(8,128)(2,1)} %text.1, bf16[256,512]{1,0:T(8,128)(2,1)} %image.1, f32[1]{0:T(128)S(6)} %copy.14.scale_ref, bf16[1024,512]{1,0:T(8,128)(2,1)} %bitcast.5, bf16[512,512]{1,0:T(8,128)(2,1)} %bitcast.6, ...), custom_call_target="tpu_custom_call" | custom-call | tf_op jit(solution)/shard_map/pallas_call | solution.py:453
  108.3 0.0 copy-start
  108.4 1.7 %copy.15 = bf16[256,512]{1,0:T(8,128)(2,1)} copy(bf16[256,512]{1,0:T(8,128)(2,1)} %get-tuple-element.16) | data formatting | bytes 524288
  110.1 0.0 copy-done
  110.1 0.0 copy-start.2
  110.1 0.8 copy.16
  110.9 0.1 copy-done.2
  110.9 0.0 copy-start.1
  110.9 0.6 copy.17
  111.6 0.2 copy-done.1
  111.8 0.6 copy.18
Async XLA Ops:
  108.3 1.7 %copy-start = (bf16[1024,256]{1,0:T(8,128)(2,1)S(1)}, bf16[1024,256]{1,0:T(8,128)(2,1)}, u32[]{:S(2)}) copy-start(bf16[1024,256]{1,0:T(8,128)(2,1)} %get-tuple-element.17) | copy-start | bytes 1572868
  110.1 0.9 copy-start.2
  110.9 0.9 copy-start.1

commit v2 on v1

--- a/solution.py
+++ b/solution.py
@@ -12,6 +12,7 @@
 LOG2E = 1.4426950408889634
 LANES = 128
 CORES = 2
+RING = 4
 
 
 def unit_rows(values):
@@ -48,10 +49,10 @@
     def kernel(
         text, image, scale_ref, hidden, w_in, w_out,
         image_out, input_out, first_out, second_out,
-        text_low, cols, scores, sgrad, row_max, row_lse, col_lse, row_st, row_rx, col_st, col_rx,
+        text_low, cols, scores, sgrad, row_max, row_sum, row_lse, col_lse, row_st, row_rx, col_st, col_rx,
         wi_all, wo_all, h_own, t_full, t_keep, t_sx, t_sr, t_tx, t_rx,
         g_st, g_all, g_acc, in_st, act_all, slope_all, pre_all,
-        w_tx, w_rx, i_tx, i_rx,
+        w_tx, w_rx, i_tx, i_rx, i_own,
         gat_s, gat_r, cs_s, cs_r, rs_s, rs_r, ww_s, ww_r, h_s, h_r,
         ts_s, ts_r, tc_s, tc_r, gs_s, gs_r, gr_s, in_s, in_r, ir_s,
         w_s, w_r, im_s, im_r, io_s, io_r,
@@ -88,6 +89,19 @@
         def arrived(ref, recv):
             copy(ref, ref, h_s, recv, at(spot, sib)).wait_recv()
 
+        def shift(step):
+            dz, dy = step[0] % RING, step[1] % RING
+            z = lax.rem(d // RING + dz, RING)
+            return z * RING + lax.rem(lax.rem(d, RING) + dy, RING)
+
+        def slot(step):
+            return (step[0] % RING) * RING + step[1] % RING
+
+        steps = [(a, b) for a in range(RING) for b in range(RING)]
+
+        def away(step):
+            return (-step[0] % RING, -step[1] % RING)
+
         def others(mine, count):
             return [lax.rem(mine + k, count) for k in range(1, count)]
 
@@ -111,15 +125,42 @@
                     device_id_type=MESH,
                 )
             own_unit, _ = unit_rows(image[tile(s, half), :])
-            cols[tile(d, half), :] = own_unit.astype(BF16)
+            cols[0:half, :] = own_unit.astype(BF16)
             h_own[s] = hidden[tile(e, chunk), :]
             wi_all[e] = w_in[...]
             wo_all[e] = w_out[...]
             pl.semaphore_wait(barrier, n_dp + n_el - 2)
 
-        for p in others(d, n_dp):
-            push(cols.at[tile(d, half), :], cols.at[tile(d, half), :], gat_s.at[p], gat_r.at[d],
-                 {"dp": p})
+        quarter = half // 4
+        spans = {"A": (0, 2), "B": (2, 2), "A0": (0, 1), "A1": (1, 1), "B0": (2, 1), "B1": (3, 1)}
+        ahead = {"Y-": (0, -1), "Y+": (0, 1), "Z-": (-1, 0), "Z+": (1, 0)}
+        passed = []
+
+        def piece_of(step, name):
+            first, count = spans[name]
+            base = slot(step) * half + first * quarter
+            return cols.at[base : base + count * quarter, :]
+
+        def forward(step, name, *directions):
+            for way in directions:
+                move = ahead[way]
+                lands = (step[0] - move[0], step[1] - move[1])
+                c = copy(piece_of(step, name), piece_of(lands, name), gat_s.at[len(passed)],
+                         gat_r.at[slot(lands), spans[name][0]], {"dp": shift(move)})
+                c.start()
+                passed.append(c)
+
+        def landed(step, name):
+            arrived(piece_of(step, name), gat_r.at[slot(step), spans[name][0]])
+
+        for way in ("Y-", "Y+"):
+            forward((0, 0), "A", way)
+        for way in ("Z-", "Z+"):
+            forward((0, 0), "B", way)
+        for way in ("Y-", "Y+"):
+            forward((0, 0), "B", way)
+        for way in ("Z-", "Z+"):
+            forward((0, 0), "A", way)
 
         mate = (1 - s) * n_mp + m
         push(hidden.at[tile(mate, chunk), :], h_own.at[s], h_s, h_r, {"section": 1 - s})
@@ -157,35 +198,109 @@
                 act_all[tile(r, pair), :] = (pre * sigm).astype(BF16)
                 slope_all[tile(r, pair), :] = sigm + GELU * pre * sigm * (1.0 - sigm)
 
-        row_max[...] = jnp.full(row_max.shape, -1e30, F32)
-
-        def block_scores(p):
-            piece = cols[tile(p, half), :]
-
-            def part(r, peak):
-                value = mult2 * dot_nt(text_low[tile(r, pair), :], piece)
-                scores[p, tile(r, pair), :] = value
-                row_max[tile(r, pair), :] = jnp.maximum(row_max[tile(r, pair), :], value)
-                return jnp.maximum(peak, jnp.max(value, axis=0, keepdims=True))
-
-            peak = lax.fori_loop(0, line, part, jnp.full((1, half), -1e30, F32))
-
-            def total(r, acc):
-                value = scores[p, tile(r, pair), :]
-                return acc + jnp.sum(jnp.exp2(value - peak), axis=0, keepdims=True)
-
-            acc = lax.fori_loop(0, line, total, jnp.zeros((1, half), F32))
-            col_st[pl.ds(p, 1), :] = peak
-            col_st[pl.ds(n_dp + p, 1), :] = acc
+        def pair_scores(one, two, fresh):
+            piece = jnp.concatenate(
+                [cols[slot(k) * half : (slot(k) + 1) * half, :] for k in (one, two)], axis=0)
+            peak = total = None
+            for r in range(line):
+                part = pl.ds(r * pair, pair)
+                value = mult2 * dot_nt(text_low[part, :], piece)
+                left, right = value[:, 0:half], value[:, half : 2 * half]
+                scores[slot(one), part, :] = left
+                scores[slot(two), part, :] = right
+                best = jnp.maximum(left, right)
+                if not fresh:
+                    best = jnp.maximum(best, row_max[part, :])
+                mass = jnp.exp2(left - best) + jnp.exp2(right - best)
+                if not fresh:
+                    mass = mass + row_sum[part, :] * jnp.exp2(row_max[part, :] - best)
+                row_max[part, :] = best
+                row_sum[part, :] = mass
+                top = jnp.max(value, axis=0, keepdims=True)
+                if peak is None:
+                    peak = top
+                    total = jnp.sum(jnp.exp2(value - peak), axis=0, keepdims=True)
+                else:
+                    top = jnp.maximum(peak, top)
+                    total = total * jnp.exp2(peak - top) + jnp.sum(
+                        jnp.exp2(value - top), axis=0, keepdims=True)
+                    peak = top
+            for k, step in enumerate((one, two)):
+                p = shift(step)
+                col_st[pl.ds(p, 1), :] = peak[:, k * half : (k + 1) * half]
+                col_st[pl.ds(n_dp + p, 1), :] = total[:, k * half : (k + 1) * half]
 
         with jax.named_scope("c_blocks"):
-            block_scores(d)
-            for k, p in enumerate(sources(d, n_dp)):
-                arrived(cols.at[tile(p, half), :], gat_r.at[p])
-                block_scores(p)
-                if k == n_dp // 2:
-                    relay_weight(0, 1, 4, line - 1)
-                    relay_weight(1, line - 1, 4, 1)
+            landed((0, 1), "A")
+            forward((0, 1), "A0", "Y-")
+            forward((0, 1), "A", "Z-", "Z+")
+            landed((1, 0), "B")
+            forward((1, 0), "B0", "Z-")
+            forward((1, 0), "B", "Y-", "Y+")
+            landed((0, 3), "A")
+            forward((0, 3), "A1", "Y+")
+            forward((0, 3), "A", "Z-", "Z+")
+            landed((3, 0), "B")
+            forward((3, 0), "B1", "Z+")
+            forward((3, 0), "B", "Y-", "Y+")
+            landed((0, 1), "B")
+            forward((0, 1), "B0", "Y-")
+            landed((1, 0), "A")
+            forward((1, 0), "A0", "Z-")
+            landed((0, 3), "B")
+            forward((0, 3), "B1", "Y+")
+            landed((3, 0), "A")
+            forward((3, 0), "A1", "Z+")
+            pair_scores((0, 0), (0, 1), True)
+            for name, way in (("A0", "Y-"), ("A1", "Y+")):
+                landed((0, 2), name)
+                forward((0, 2), name, "Z-", "Z+")
+            for name in ("B0", "B1"):
+                landed((2, 0), name)
+                forward((2, 0), name, "Y-", "Y+")
+            pair_scores((0, 3), (1, 0), False)
+            for dy in (1, 3):
+                landed((1, dy), "A")
+                forward((1, dy), "A0", "Z-")
+                landed((3, dy), "A")
+                forward((3, dy), "A1", "Z+")
+            for dz in (1, 3):
+                landed((dz, 1), "B")
+                forward((dz, 1), "B0", "Y-")
+                landed((dz, 3), "B")
+                forward((dz, 3), "B1", "Y+")
+            pair_scores((3, 0), (1, 1), False)
+            relay_weight(0, 1, 4, line - 1)
+            relay_weight(1, line - 1, 4, 1)
+            for name in ("A0", "A1"):
+                landed((1, 2), name)
+                landed((3, 2), name)
+            forward((1, 2), "A0", "Z-")
+            forward((3, 2), "A1", "Z+")
+            for name in ("B0", "B1"):
+                landed((2, 1), name)
+                landed((2, 3), name)
+            forward((2, 1), "B0", "Y-")
+            forward((2, 3), "B1", "Y+")
+            pair_scores((1, 3), (3, 1), False)
+            for name in ("B0", "B1"):
+                landed((0, 2), name)
+            for name in ("A0", "A1"):
+                landed((2, 0), name)
+            pair_scores((3, 3), (0, 2), False)
+            for name in ("B0", "B1"):
+                landed((1, 2), name)
+            pair_scores((2, 0), (1, 2), False)
+            for name in ("B0", "B1"):
+                landed((3, 2), name)
+            for name in ("A0", "A1"):
+                landed((2, 1), name)
+            pair_scores((3, 2), (2, 1), False)
+            for name in ("A0", "A1"):
+                landed((2, 3), name)
+            for name in ("A0", "A1", "B0", "B1"):
+                landed((2, 2), name)
+            pair_scores((2, 3), (2, 2), False)
 
         with jax.named_scope("d_colsend"):
             col_rx[d] = col_st[...]
@@ -196,12 +311,8 @@
             for r in range(n_el):
                 part = pl.ds(r * chunk, chunk)
                 peak = jnp.max(row_max[part, :], axis=1, keepdims=True)
-
-                def total(p, acc):
-                    return acc + jnp.exp2(scores[p, part, :] - peak)
-
-                acc = lax.fori_loop(0, n_dp, total, jnp.zeros((chunk, LANES), F32))
-                acc = jnp.sum(acc, axis=1, keepdims=True)
+                acc = jnp.sum(row_sum[part, :] * jnp.exp2(row_max[part, :] - peak), axis=1,
+                              keepdims=True)
                 row_st[r : r + 1, :] = jnp.broadcast_to(peak, (chunk, LANES)).T[0:1, :]
                 row_st[n_el + r : n_el + r + 1, :] = jnp.broadcast_to(acc, (chunk, LANES)).T[0:1, :]
             row_rx[e] = row_st[...]
@@ -235,21 +346,22 @@
 
         def score_rows(r):
             base = row_lse[tile(r, pair), :]
-            for p in range(n_dp):
-                value = scores[p, tile(r, pair), :]
-                both = jnp.exp2(value - base) + jnp.exp2(value - col_lse[p : p + 1, :])
-                sgrad[tile(r, pair), p * half : (p + 1) * half] = both.astype(BF16)
+            for step in steps:
+                k = slot(step)
+                value = scores[k, tile(r, pair), :]
+                low = col_lse[pl.ds(shift(step), 1), :]
+                both = jnp.exp2(value - base) + jnp.exp2(value - low)
+                sgrad[tile(r, pair), k * half : (k + 1) * half] = both.astype(BF16)
 
             @pl.when(r == m)
             def _():
                 line_at = tile(m * n_sec + s, half)
-                value = scores[d, line_at, :]
+                value = scores[0, line_at, :]
                 both = jnp.exp2(value - row_lse[line_at, :]) + jnp.exp2(
                     value - col_lse[pl.ds(d, 1), :])
                 diagonal = lax.broadcasted_iota(jnp.int32, (half, half), 0) == (
                     lax.broadcasted_iota(jnp.int32, (half, half), 1))
-                sgrad[line_at, tile(d, half)] = (
-                    both - jnp.where(diagonal, 1.0, 0.0)).astype(BF16)
+                sgrad[line_at, 0:half] = (both - jnp.where(diagonal, 1.0, 0.0)).astype(BF16)
 
         def join(where):
             arrived(t_sr.at[where], ts_r.at[where])
@@ -275,13 +387,17 @@
                     push(t_tx.at[last], t_rx.at[spot], tc_s.at[i], tc_r.at[spot],
                          at(last, core))
 
-        def image_part(p):
-            return dot_tn(sgrad[:, tile(p, half)], text_low[...])
-
         with jax.named_scope("h_image"):
-            for p in others(d, n_dp):
-                i_tx[p] = image_part(p).astype(BF16)
-                push(i_tx.at[p], i_rx.at[d], im_s.at[p], im_r.at[d], {"dp": p})
+            for g in range(RING):
+                part = dot_tn(sgrad[:, g * RING * half : (g + 1) * RING * half], text_low[...])
+                for k in range(RING):
+                    step = (g, k)
+                    if step == (0, 0):
+                        i_own[...] = part[0:half, :]
+                        continue
+                    i_tx[slot(step)] = part[k * half : (k + 1) * half, :].astype(BF16)
+                    push(i_tx.at[slot(step)], i_rx.at[slot(away(step))], im_s.at[slot(step)],
+                         im_r.at[slot(away(step))], {"dp": shift(step)})
 
         mine = tile(e, chunk)
 
@@ -336,8 +452,7 @@
             spread(layer)
             g_acc[...] = g_st[layer].astype(F32)
 
-            @pl.loop(0, n_mp)
-            def _(j):
+            for j in range(n_mp):
                 index = layer * n_mp + j
                 pre = dot_nn(h_own[layer], wi_all[index])
                 back = dot_nt(g_st[layer], wo_all[index])
@@ -406,10 +521,10 @@
 
         with jax.named_scope("p_image"):
             image_half = tile(s, half)
-            total = image_part(d)
-            for p in sources(d, n_dp):
-                arrived(i_rx.at[p], im_r.at[p])
-                total = total + i_rx[p].astype(F32)
+            total = i_own[...]
+            for k in range(1, n_dp):
+                arrived(i_rx.at[k], im_r.at[k])
+                total = total + i_rx[k].astype(F32)
             unit, length = unit_rows(image[image_half, :])
             image_out[image_half, :] = unit_backward(unit, length, mult * total).astype(BF16)
             push(image_out.at[image_half, :], image_out.at[image_half, :], io_s, io_r,
@@ -428,7 +543,7 @@
                 index = far(step) * CORES + sib
                 arrived(slab(index), in_r.at[index])
             arrived(image_out.at[tile(1 - s, half), :], io_r)
-            for c in sent:
+            for c in sent + passed:
                 c.wait_send()
             for layer in range(n_sec):
                 drain_spread(layer)
@@ -467,6 +582,7 @@
                 pltpu.VMEM((rows, columns), BF16),
                 pltpu.VMEM((rows, LANES), F32),
                 pltpu.VMEM((rows, LANES), F32),
+                pltpu.VMEM((rows, LANES), F32),
                 pltpu.VMEM((n_dp, half), F32),
                 pltpu.VMEM((2 * n_el, chunk), F32),
                 pltpu.VMEM((n_el, 2 * n_el, chunk), F32),
@@ -492,7 +608,8 @@
                 pltpu.VMEM((n_dp, 2, share, hid), BF16),
                 pltpu.VMEM((n_dp, half, feats), BF16),
                 pltpu.VMEM((n_dp, half, feats), BF16),
-                dma((n_dp,)), dma((n_dp,)),
+                pltpu.VMEM((half, feats), F32),
+                dma((44,)), dma((n_dp, 4)),
                 dma((n_dp,)), dma((n_dp,)),
                 dma((n_el,)), dma((n_el,)),
                 dma((2, 7)), dma((2, n_el)),

time: 113 us -> 110 us (0.973)
  Pallas kernels: 107 us -> 103 us
    pallas_call x1, Pallas kernels: 107 us -> 103 us  [body(): pl.pallas_call(make_kernel(n_sec, n_dp, n_mp), out_shape=(jax.ShapeDtypeS...]
where the time goes in v2:
time: 110 us; the launch traced here: 109 us
  Pallas kernels  103 us (94%)
  local copies, waits for them, and re-layouts  4.08 us (4%)
  between operations  1.3 us (1%)
    pallas_call x1, Pallas kernels, body(): pl.pallas_call(make_kernel(n_sec, n_dp, n_mp), out_shape=(jax.ShapeDtypeS...  103 us
    unnamed x10, local copies, waits for them, and re-layouts  4.08 us

profile of v2, /device:TPU:0, one launch (start us, length us, event | category | flops | bytes accessed | tf_op | source)
XLA Modules:
  0.0 108.6 jit_solution(11115639421997163915)
XLA Ops:
  1.3 103.2 %shard_map.93 = (bf16[256,512]{1,0:T(8,128)(2,1)}, bf16[1024,256]{1,0:T(8,128)(2,1)}, f32[32,512]{1,0:T(8,128)}, f32[32,512]{1,0:T(8,128)}) custom-call(bf16[1024,512]{1,0:T(8,128)(2,1)} %text.1, bf16[256,512]{1,0:T(8,128)(2,1)} %image.1, f32[1]{0:T(128)S(6)} %copy.14.scale_ref, bf16[1024,512]{1,0:T(8,128)(2,1)} %bitcast.5, bf16[512,512]{1,0:T(8,128)(2,1)} %bitcast.6, ...), custom_call_target="tpu_custom_call" | custom-call | tf_op jit(solution)/shard_map/pallas_call | solution.py:568
  104.5 0.0 copy-start
  104.5 1.7 %copy.15 = bf16[256,512]{1,0:T(8,128)(2,1)} copy(bf16[256,512]{1,0:T(8,128)(2,1)} %get-tuple-element.16) | data formatting | bytes 524288
  106.2 0.0 copy-done
  106.2 0.0 copy-start.2
  106.2 0.8 copy.16
  107.0 0.1 copy-done.2
  107.1 0.0 copy-start.1
  107.1 0.6 copy.17
  107.7 0.2 copy-done.1
  107.9 0.6 copy.18
Async XLA Ops:
  104.5 1.7 %copy-start = (bf16[1024,256]{1,0:T(8,128)(2,1)S(1)}, bf16[1024,256]{1,0:T(8,128)(2,1)}, u32[]{:S(2)}) copy-start(bf16[1024,256]{1,0:T(8,128)(2,1)} %get-tuple-element.17) | copy-start | bytes 1572868
  106.2 0.9 copy-start.2
  107.1 0.9 copy-start.1

commit v3 on v2

--- a/solution.py
+++ b/solution.py
@@ -52,10 +52,10 @@
         text_low, cols, scores, sgrad, row_max, row_sum, row_lse, col_lse, row_st, row_rx, col_st, col_rx,
         wi_all, wo_all, h_own, t_full, t_keep, t_sx, t_sr, t_tx, t_rx,
         g_st, g_all, g_acc, in_st, act_all, slope_all, pre_all,
-        w_tx, w_rx, i_tx, i_rx, i_own,
+        w_full, w_tx, w_rx, w_sum, w_st, w_end, i_tx, i_rx, i_own, i_st, i_end,
         gat_s, gat_r, cs_s, cs_r, rs_s, rs_r, ww_s, ww_r, h_s, h_r,
         ts_s, ts_r, tc_s, tc_r, gs_s, gs_r, gr_s, in_s, in_r, ir_s,
-        w_s, w_r, im_s, im_r, io_s, io_r,
+        wc_s, wc_r, w_s, w_r, im_s, im_r, io_s, io_r,
     ):
         s = lax.axis_index("section")
         d = lax.axis_index("dp")
@@ -165,6 +165,19 @@
         mate = (1 - s) * n_mp + m
         push(hidden.at[tile(mate, chunk), :], h_own.at[s], h_s, h_r, {"section": 1 - s})
         ww = ((w_in, wi_all), (w_out, wo_all))
+        z_at, y_at = d // RING, lax.rem(d, RING)
+        cell = (z_at * RING + y_at, y_at * RING + z_at)
+        band = (z_at, y_at)
+        cross = far(2) * CORES + core
+        bit = w_in.shape[0] // n_dp
+
+        def along(which, step):
+            return {"dp": shift((0, step) if which == 0 else (step, 0))}
+
+        for which in (0, 1):
+            part = tile(cell[which], bit)
+            push(ww[which][0].at[part, :], ww[which][1].at[e, part, :], wc_s.at[which, 0],
+                 wc_r.at[which, 0], at(far(2), core))
         for which in (0, 1):
             push(ww[which][0], ww[which][1].at[e], ww_s.at[which, 1], ww_r.at[which, e],
                  at(far(line - 1), core))
@@ -174,12 +187,34 @@
             push(ww[which][0], ww[which][1].at[e], ww_s.at[which, 0], ww_r.at[which, e],
                  at(spot, sib))
 
-        def relay_weight(which, step, slot, onward=None):
+        def cross_first(which):
+            mine_bit = ww[which][1].at[cross, tile(cell[which], bit), :]
+            arrived(mine_bit, wc_r.at[which, 0])
+            for k in range(1, RING):
+                push(mine_bit, mine_bit, wc_s.at[which, k], wc_r.at[which, RING - k],
+                     along(which, k))
+
+        def cross_second(which):
+            for k in range(1, RING):
+                other = band[which] * RING + lax.rem(band[1 - which] + k, RING)
+                arrived(ww[which][1].at[cross, tile(other, bit), :], wc_r.at[which, k])
+            group = ww[which][1].at[cross, tile(band[which], RING * bit), :]
+            for k in range(1, RING):
+                push(group, group, wc_s.at[which, RING + k], wc_r.at[which, 2 * RING - k],
+                     along(1 - which, k))
+
+        def cross_third(which):
+            for k in range(1, RING):
+                other = lax.rem(band[which] + k, RING)
+                arrived(ww[which][1].at[cross, tile(other, RING * bit), :],
+                        wc_r.at[which, RING + k])
+            push(ww[which][1].at[cross], ww[which][1].at[cross], ww_s.at[which, 6],
+                 ww_r.at[which, cross], at(spot, sib))
+
+        def relay_weight(which, step, slot):
             index = far(step) * CORES + core
             buf = ww[which][1].at[index]
             arrived(buf, ww_r.at[which, index])
-            if onward is not None:
-                push(buf, buf, ww_s.at[which, 3], ww_r.at[which, index], at(far(onward), core))
             push(buf, buf, ww_s.at[which, slot], ww_r.at[which, index], at(spot, sib))
 
         def sigmoid(pre):
@@ -270,8 +305,8 @@
                 landed((dz, 3), "B")
                 forward((dz, 3), "B1", "Y+")
             pair_scores((3, 0), (1, 1), False)
-            relay_weight(0, 1, 4, line - 1)
-            relay_weight(1, line - 1, 4, 1)
+            cross_first(0)
+            cross_first(1)
             for name in ("A0", "A1"):
                 landed((1, 2), name)
                 landed((3, 2), name)
@@ -329,9 +364,9 @@
                 acc = acc + rx[k, n : 2 * n, :] * jnp.exp2(rx[k, 0:n, :] - peak)
             return peak + (jnp.log(acc) * LOG2E + 1.0)
 
-        with jax.named_scope("f_relay"):
-            relay_weight(1, 1, 5)
-            relay_weight(0, line - 1, 5)
+        with jax.named_scope("f_cross"):
+            cross_second(0)
+            cross_second(1)
 
         with jax.named_scope("f_merge"):
             for p in sources(d, n_dp):
@@ -387,19 +422,56 @@
                     push(t_tx.at[last], t_rx.at[spot], tc_s.at[i], tc_r.at[spot],
                          at(last, core))
 
+        with jax.named_scope("g_relay"):
+            relay_weight(1, 1, 3)
+            relay_weight(0, line - 1, 3)
+            relay_weight(0, 1, 4)
+            relay_weight(1, line - 1, 4)
+
+        fold = half // 2
+
         with jax.named_scope("h_image"):
-            for g in range(RING):
+            for g in (2, 1, 3, 0):
                 part = dot_tn(sgrad[:, g * RING * half : (g + 1) * RING * half], text_low[...])
                 for k in range(RING):
-                    step = (g, k)
-                    if step == (0, 0):
-                        i_own[...] = part[0:half, :]
-                        continue
-                    i_tx[slot(step)] = part[k * half : (k + 1) * half, :].astype(BF16)
-                    push(i_tx.at[slot(step)], i_rx.at[slot(away(step))], im_s.at[slot(step)],
-                         im_r.at[slot(away(step))], {"dp": shift(step)})
+                    low = part[k * half : k * half + fold, :]
+                    high = part[k * half + fold : (k + 1) * half, :]
+                    if g == 0:
+                        i_own[0, k] = low
+                    else:
+                        i_tx[0, g, k] = low.astype(BF16)
+                    if k == 0:
+                        i_own[1, g] = high
+                    else:
+                        i_tx[1, k, g] = high.astype(BF16)
+                if g > 0:
+                    push(i_tx.at[0, g], i_rx.at[0, RING - g], im_s.at[0, g], im_r.at[0, RING - g],
+                         along(1, g))
+            for k in (2, 1, 3):
+                push(i_tx.at[1, k], i_rx.at[1, RING - k], im_s.at[1, k], im_r.at[1, RING - k],
+                     along(0, k))
+
+        def image_second():
+            for which in (0, 1):
+                for k in (1, 3, 2):
+                    arrived(i_rx.at[which, k], im_r.at[which, k])
+                for g in (2, 1, 3, 0):
+                    total = i_own[which, g]
+                    for k in range(1, RING):
+                        total = total + i_rx[which, k, g].astype(F32)
+                    if g == 0:
+                        i_own[which, 0] = total
+                    else:
+                        i_st[which, g] = total.astype(BF16)
+                        push(i_st.at[which, g], i_end.at[which, RING - g],
+                             im_s.at[which, RING + g], im_r.at[which, 2 * RING - g],
+                             along(which, g))
 
         mine = tile(e, chunk)
+
+        with jax.named_scope("h_cross"):
+            cross_third(0)
+            cross_third(1)
 
         with jax.named_scope("i_topgrad"):
             total = join(spot)
@@ -412,8 +484,6 @@
 
         with jax.named_scope("j_weights"):
             arrived(h_own.at[1 - s], h_r)
-            relay_weight(0, 2, 6)
-            relay_weight(1, 2, 6)
             for step in range(line):
                 index = far(step) * CORES + sib
                 for which in (0, 1):
@@ -498,19 +568,42 @@
                 weight_rows(index)
 
         def send_weights(which):
-            for p in others(d, n_dp):
-                push(w_tx.at[p, which], w_rx.at[d, which], w_s.at[which, p], w_r.at[which, d],
-                     {"dp": p})
+            for k in (2, 1, 3):
+                other = lax.rem(band[which] + k, RING)
+                push(w_tx.at[which, tile(other, RING * share), :], w_rx.at[which, RING - k],
+                     w_s.at[which, k], w_r.at[which, RING - k], along(1 - which, k))
+
+        def weight_second(which):
+            total = w_full[which, tile(band[which], RING * share), :]
+            for k in (1, 3, 2):
+                arrived(w_rx.at[which, k], w_r.at[which, k])
+                total = total + w_rx[which, k].astype(F32)
+            w_sum[which] = total
+            w_st[which] = total.astype(BF16)
+            for k in (2, 1, 3):
+                other = lax.rem(band[1 - which] + k, RING)
+                push(w_st.at[which, tile(other, share), :], w_end.at[which, RING - k],
+                     w_s.at[which, RING + k], w_r.at[which, 2 * RING - k], along(which, k))
+
+        def weight_last(which, out):
+            total = w_sum[which, tile(band[1 - which], share), :]
+            for k in (1, 3, 2):
+                arrived(w_end.at[which, k], w_r.at[which, RING + k])
+                total = total + w_end[which, k].astype(F32)
+            out[...] = total
 
         with jax.named_scope("n_wgrad"):
             g_rows = g_all[...].reshape(rows, feats)
-            grad_second = dot_tn(g_rows, act_all[...])
+            grad = dot_tn(g_rows, act_all[...])
             for p in range(n_dp):
-                w_tx[p, 1] = grad_second[p * share : (p + 1) * share, :].astype(BF16)
+                q = (p % RING) * RING + p // RING
+                w_full[1, q * share : (q + 1) * share, :] = grad[p * share : (p + 1) * share, :]
+                w_tx[1, q * share : (q + 1) * share, :] = grad[
+                    p * share : (p + 1) * share, :].astype(BF16)
             send_weights(1)
-            grad_first = dot_tn(hidden[...], pre_all[...])
-            for p in range(n_dp):
-                w_tx[p, 0] = grad_first[p * share : (p + 1) * share, :].astype(BF16)
+            grad = dot_tn(hidden[...], pre_all[...])
+            w_full[0] = grad
+            w_tx[0] = grad.astype(BF16)
             send_weights(0)
 
         with jax.named_scope("o_inrelay"):
@@ -519,24 +612,29 @@
                 arrived(slab(index), in_r.at[index])
                 push(slab(index), slab(index), ir_s.at[hop], in_r.at[index], at(spot, sib))
 
-        with jax.named_scope("p_image"):
+        with jax.named_scope("p_second"):
+            image_second()
+        with jax.named_scope("p_wsecond"):
+            weight_second(1)
+            weight_second(0)
+
+        with jax.named_scope("q_image"):
             image_half = tile(s, half)
-            total = i_own[...]
-            for k in range(1, n_dp):
-                arrived(i_rx.at[k], im_r.at[k])
-                total = total + i_rx[k].astype(F32)
             unit, length = unit_rows(image[image_half, :])
-            image_out[image_half, :] = unit_backward(unit, length, mult * total).astype(BF16)
+            for which in (0, 1):
+                total = i_own[which, 0]
+                for k in (1, 3, 2):
+                    arrived(i_end.at[which, k], im_r.at[which, RING + k])
+                    total = total + i_end[which, k].astype(F32)
+                part = slice(which * fold, (which + 1) * fold)
+                image_out[tile(2 * s + which, fold), :] = unit_backward(
+                    unit[part, :], length[part, :], mult * total).astype(BF16)
             push(image_out.at[image_half, :], image_out.at[image_half, :], io_s, io_r,
                  {"section": 1 - s})
 
         with jax.named_scope("q_wsum"):
-            for which, out in ((1, second_out), (0, first_out)):
-                total = w_tx[d, which].astype(F32)
-                for p in sources(d, n_dp):
-                    arrived(w_rx.at[p, which], w_r.at[which, p])
-                    total = total + w_rx[p, which].astype(F32)
-                out[...] = total
+            weight_last(1, second_out)
+            weight_last(0, first_out)
 
         with jax.named_scope("r_drain"):
             for step in range(line):
@@ -604,11 +702,17 @@
                 pltpu.VMEM((rows, hid), BF16),
                 pltpu.VMEM((rows, hid), F32),
                 pltpu.VMEM((rows, hid), BF16),
-                pltpu.VMEM((n_dp, 2, share, hid), BF16),
-                pltpu.VMEM((n_dp, 2, share, hid), BF16),
-                pltpu.VMEM((n_dp, half, feats), BF16),
-                pltpu.VMEM((n_dp, half, feats), BF16),
-                pltpu.VMEM((half, feats), F32),
+                pltpu.VMEM((2, feats, hid), F32),
+                pltpu.VMEM((2, feats, hid), BF16),
+                pltpu.VMEM((2, RING, RING * share, hid), BF16),
+                pltpu.VMEM((2, RING * share, hid), F32),
+                pltpu.VMEM((2, RING * share, hid), BF16),
+                pltpu.VMEM((2, RING, share, hid), BF16),
+                pltpu.VMEM((2, RING, RING, half // 2, feats), BF16),
+                pltpu.VMEM((2, RING, RING, half // 2, feats), BF16),
+                pltpu.VMEM((2, RING, half // 2, feats), F32),
+                pltpu.VMEM((2, RING, half // 2, feats), BF16),
+                pltpu.VMEM((2, RING, half // 2, feats), BF16),
                 dma((44,)), dma((n_dp, 4)),
                 dma((n_dp,)), dma((n_dp,)),
                 dma((n_el,)), dma((n_el,)),
@@ -620,8 +724,9 @@
                 dma((line,)),
                 dma((line,)), dma((n_el,)),
                 dma((line,)),
-                dma((2, n_dp)), dma((2, n_dp)),
-                dma((n_dp,)), dma((n_dp,)),
+                dma((2, 2 * RING)), dma((2, 2 * RING)),
+                dma((2, 2 * RING)), dma((2, 2 * RING)),
+                dma((2, 2 * RING)), dma((2, 2 * RING)),
                 dma, dma,
             ],
             compiler_params=pltpu.CompilerParams(

time: 110 us -> 90.3 us (0.82)
  Pallas kernels: 103 us -> 83.6 us
    pallas_call x1, Pallas kernels: 103 us -> 83.6 us  [body(): pl.pallas_call(make_kernel(n_sec, n_dp, n_mp), out_shape=(jax.ShapeDtypeS...]
where the time goes in v3:
time: 90.3 us; the launch traced here: 89 us
  Pallas kernels  83.6 us (93%)
  local copies, waits for them, and re-layouts  4.08 us (5%)
  between operations  1.3 us (1%)
    pallas_call x1, Pallas kernels, body(): pl.pallas_call(make_kernel(n_sec, n_dp, n_mp), out_shape=(jax.ShapeDtypeS...  83.6 us
    unnamed x10, local copies, waits for them, and re-layouts  4.08 us

profile of v3, /device:TPU:0, one launch (start us, length us, event | category | flops | bytes accessed | tf_op | source)
XLA Modules:
  0.0 89.0 jit_solution(755270480784602488)
XLA Ops:
  1.3 83.6 %shard_map.93 = (bf16[256,512]{1,0:T(8,128)(2,1)}, bf16[1024,256]{1,0:T(8,128)(2,1)}, f32[32,512]{1,0:T(8,128)}, f32[32,512]{1,0:T(8,128)}) custom-call(bf16[1024,512]{1,0:T(8,128)(2,1)} %text.1, bf16[256,512]{1,0:T(8,128)(2,1)} %image.1, f32[1]{0:T(128)S(6)} %copy.14.scale_ref, bf16[1024,512]{1,0:T(8,128)(2,1)} %bitcast.5, bf16[512,512]{1,0:T(8,128)(2,1)} %bitcast.6, ...), custom_call_target="tpu_custom_call" | custom-call | tf_op jit(solution)/shard_map/pallas_call | solution.py:666
  84.9 0.0 copy-start
  84.9 1.7 %copy.15 = bf16[256,512]{1,0:T(8,128)(2,1)} copy(bf16[256,512]{1,0:T(8,128)(2,1)} %get-tuple-element.16) | data formatting | bytes 524288
  86.6 0.0 copy-done
  86.6 0.0 copy-start.2
  86.6 0.8 copy.16
  87.4 0.1 copy-done.2
  87.5 0.0 copy-start.1
  87.5 0.6 copy.17
  88.1 0.2 copy-done.1
  88.3 0.6 copy.18
Async XLA Ops:
  84.9 1.7 %copy-start = (bf16[1024,256]{1,0:T(8,128)(2,1)S(1)}, bf16[1024,256]{1,0:T(8,128)(2,1)}, u32[]{:S(2)}) copy-start(bf16[1024,256]{1,0:T(8,128)(2,1)} %get-tuple-element.17) | copy-start | bytes 1572868
  86.6 0.9 copy-start.2
  87.5 0.9 copy-start.1

commit v4 on v3

--- a/solution.py
+++ b/solution.py
@@ -51,7 +51,7 @@
         image_out, input_out, first_out, second_out,
         text_low, cols, scores, sgrad, row_max, row_sum, row_lse, col_lse, row_st, row_rx, col_st, col_rx,
         wi_all, wo_all, h_own, t_full, t_keep, t_sx, t_sr, t_tx, t_rx,
-        g_st, g_all, g_acc, in_st, act_all, slope_all, pre_all,
+        g_st, g_all, slope_own, in_st, act_all, slope_all, pre_all,
         w_full, w_tx, w_rx, w_sum, w_st, w_end, i_tx, i_rx, i_own, i_st, i_end,
         gat_s, gat_r, cs_s, cs_r, rs_s, rs_r, ww_s, ww_r, h_s, h_r,
         ts_s, ts_r, tc_s, tc_r, gs_s, gs_r, gr_s, in_s, in_r, ir_s,
@@ -178,11 +178,19 @@
             part = tile(cell[which], bit)
             push(ww[which][0].at[part, :], ww[which][1].at[e, part, :], wc_s.at[which, 0],
                  wc_r.at[which, 0], at(far(2), core))
-        for which in (0, 1):
-            push(ww[which][0], ww[which][1].at[e], ww_s.at[which, 1], ww_r.at[which, e],
-                 at(far(line - 1), core))
-            push(ww[1 - which][0], ww[1 - which][1].at[e], ww_s.at[1 - which, 2],
-                 ww_r.at[1 - which, e], at(far(1), core))
+        top = pl.ds(0, w_in.shape[0] // 2)
+        rest = pl.ds(w_in.shape[0] // 2, w_in.shape[0] // 2)
+
+        def neighbour(which, toward, part, lane):
+            push(ww[which][0].at[part, :], ww[which][1].at[e, part, :], ww_s.at[which, lane],
+                 ww_r.at[which, n_el + lane], at(far(toward), core))
+
+        for part, lane in ((top, 0), (rest, 2)):
+            neighbour(0, line - 1, part, 1 + lane)
+            neighbour(1, 1, part, 2 + lane)
+        neighbour(1, line - 1, top, 1)
+        neighbour(0, 1, top, 2)
+
         for which in (0, 1):
             push(ww[which][0], ww[which][1].at[e], ww_s.at[which, 0], ww_r.at[which, e],
                  at(spot, sib))
@@ -211,11 +219,14 @@
             push(ww[which][1].at[cross], ww[which][1].at[cross], ww_s.at[which, 6],
                  ww_r.at[which, cross], at(spot, sib))
 
-        def relay_weight(which, step, slot):
+        def relay_weight(which, step):
             index = far(step) * CORES + core
             buf = ww[which][1].at[index]
-            arrived(buf, ww_r.at[which, index])
-            push(buf, buf, ww_s.at[which, slot], ww_r.at[which, index], at(spot, sib))
+            for part, lane in ((top, 0), (rest, 2)):
+                arrived(ww[which][1].at[index, part, :],
+                        ww_r.at[which, n_el + lane + (1 if step == 1 else 2)])
+            push(buf, buf, ww_s.at[which, 5 if step == 1 else 7], ww_r.at[which, index],
+                 at(spot, sib))
 
         def sigmoid(pre):
             return 1.0 / (1.0 + jnp.exp(-GELU * pre))
@@ -354,6 +365,8 @@
             for q in others(e, n_el):
                 push(row_st, row_rx.at[e], rs_s.at[q], rs_r.at[e],
                      {"section": q // n_mp, "mp": lax.rem(q, n_mp)})
+            neighbour(1, line - 1, rest, 3)
+            neighbour(0, 1, rest, 4)
 
         def merge(rx, count, n):
             peak = rx[0, 0:n, :]
@@ -423,10 +436,9 @@
                          at(last, core))
 
         with jax.named_scope("g_relay"):
-            relay_weight(1, 1, 3)
-            relay_weight(0, line - 1, 3)
-            relay_weight(0, 1, 4)
-            relay_weight(1, line - 1, 4)
+            for which in (0, 1):
+                relay_weight(which, 1)
+                relay_weight(which, line - 1)
 
         fold = half // 2
 
@@ -473,6 +485,21 @@
             cross_third(0)
             cross_third(1)
 
+        def slopes(layer):
+            for j in range(n_mp):
+                pre = dot_nn(h_own[layer], wi_all[layer * n_mp + j])
+                sigm = sigmoid(pre)
+                slope_own[layer, j] = sigm + GELU * pre * sigm * (1.0 - sigm)
+
+        with jax.named_scope("j_weights"):
+            arrived(h_own.at[1 - s], h_r)
+            for step in range(line):
+                index = far(step) * CORES + sib
+                for which in (0, 1):
+                    arrived(ww[which][1].at[index], ww_r.at[which, index])
+            for layer in range(n_sec):
+                slopes(layer)
+
         with jax.named_scope("i_topgrad"):
             total = join(spot)
             for hop in hops[:-1]:
@@ -482,13 +509,6 @@
             unit, length = unit_rows(text[mine, :])
             g_st[n_sec - 1] = unit_backward(unit, length, mult * total).astype(BF16)
 
-        with jax.named_scope("j_weights"):
-            arrived(h_own.at[1 - s], h_r)
-            for step in range(line):
-                index = far(step) * CORES + sib
-                for which in (0, 1):
-                    arrived(ww[which][1].at[index], ww_r.at[which, index])
-
         def spread(layer):
             for c in range(chips):
                 place = layer * chips + c
@@ -520,18 +540,17 @@
 
         def feed_forward(layer):
             spread(layer)
-            g_acc[...] = g_st[layer].astype(F32)
-
+            total = g_st[layer].astype(F32)
             for j in range(n_mp):
                 index = layer * n_mp + j
-                pre = dot_nn(h_own[layer], wi_all[index])
                 back = dot_nt(g_st[layer], wo_all[index])
-                sigm = sigmoid(pre)
-                grad = (back * (sigm + GELU * pre * sigm * (1.0 - sigm))).astype(BF16)
-                g_acc[...] += dot_nt(grad, wi_all[index])
-
+                grad = (back * slope_own[layer, j]).astype(BF16)
+                total = total + dot_nt(grad, wi_all[index])
             if layer > 0:
-                g_st[layer - 1] = g_acc[...].astype(BF16)
+                g_st[layer - 1] = total.astype(BF16)
+            else:
+                for t in range(n_sec):
+                    in_st[t] = total[:, t * width : (t + 1) * width].astype(BF16)
 
         def slab(k):
             return input_out.at[tile(k, chunk), :]
@@ -541,8 +560,6 @@
                 feed_forward(layer)
 
         with jax.named_scope("l_inspread"):
-            for t in range(n_sec):
-                in_st[t] = g_acc[:, t * width : (t + 1) * width].astype(BF16)
             input_out[mine, :] = in_st[s]
             push(in_st.at[s], slab(e), in_s.at[0], in_r.at[e], at(spot, sib))
             for hop in hops[:-1]:
@@ -562,6 +579,7 @@
                 push(g_all.at[index], g_all.at[index], gr_s.at[hop], gs_r.at[index],
                      at(spot, sib))
                 weight_rows(index)
+            image_second()
             for hop in (0, 1, 3, 2) if line == 4 else range(line):
                 index = far(hop) * CORES + sib
                 arrived(g_all.at[index], gs_r.at[index])
@@ -612,12 +630,6 @@
                 arrived(slab(index), in_r.at[index])
                 push(slab(index), slab(index), ir_s.at[hop], in_r.at[index], at(spot, sib))
 
-        with jax.named_scope("p_second"):
-            image_second()
-        with jax.named_scope("p_wsecond"):
-            weight_second(1)
-            weight_second(0)
-
         with jax.named_scope("q_image"):
             image_half = tile(s, half)
             unit, length = unit_rows(image[image_half, :])
@@ -631,6 +643,10 @@
                     unit[part, :], length[part, :], mult * total).astype(BF16)
             push(image_out.at[image_half, :], image_out.at[image_half, :], io_s, io_r,
                  {"section": 1 - s})
+
+        with jax.named_scope("p_wsecond"):
+            weight_second(1)
+            weight_second(0)
 
         with jax.named_scope("q_wsum"):
             weight_last(1, second_out)
@@ -697,7 +713,7 @@
                 pltpu.VMEM((line, chunk, feats), BF16),
                 pltpu.VMEM((n_sec, chunk, feats), BF16),
                 pltpu.VMEM((n_el, chunk, feats), BF16),
-                pltpu.VMEM((chunk, feats), F32),
+                pltpu.VMEM((n_sec, n_mp, chunk, hid), F32),
                 pltpu.VMEM((n_sec, chunk, feats // n_sec), BF16),
                 pltpu.VMEM((rows, hid), BF16),
                 pltpu.VMEM((rows, hid), F32),
@@ -716,7 +732,7 @@
                 dma((44,)), dma((n_dp, 4)),
                 dma((n_dp,)), dma((n_dp,)),
                 dma((n_el,)), dma((n_el,)),
-                dma((2, 7)), dma((2, n_el)),
+                dma((2, 8)), dma((2, n_el + 5)),
                 dma, dma,
                 dma((line,)), dma((line,)),
                 dma((line,)), dma((line,)),
@@ -730,7 +746,7 @@
                 dma, dma,
             ],
             compiler_params=pltpu.CompilerParams(
-                collective_id=0, has_side_effects=True, vmem_limit_bytes=63000000
+                collective_id=0, has_side_effects=True, vmem_limit_bytes=52000000
             ),
         )(text, image, scale, hidden[0], w_in[0], w_out[0])
         image_grad, input_grad, first, second = out

time: 90.3 us -> 85.3 us (0.945); the launches traced: 89 us -> 85 us
  Pallas kernels: 83.6 us -> 75.5 us
  local copies, waits for them, and re-layouts: 4.08 us -> 8.23 us
    pallas_call x1, Pallas kernels: 83.6 us -> 75.5 us  [body(): pl.pallas_call(make_kernel(n_sec, n_dp, n_mp), out_shape=(jax.ShapeDtypeS...]
    unnamed x10 -> x14, local copies, waits for them, and re-layouts: 4.08 us -> 8.23 us
where the time goes in v4:
time: 85.3 us; the launch traced here: 85 us
  Pallas kernels  75.5 us (89%)
  local copies, waits for them, and re-layouts  8.23 us (10%)
  between operations  1.3 us (2%)
    pallas_call x1, Pallas kernels, body(): pl.pallas_call(make_kernel(n_sec, n_dp, n_mp), out_shape=(jax.ShapeDtypeS...  75.5 us
    unnamed x14, local copies, waits for them, and re-layouts  8.23 us

profile of v4, /device:TPU:0, one launch (start us, length us, event | category | flops | bytes accessed | tf_op | source)
XLA Modules:
  0.0 85.0 jit_solution(15695547758183875017)
XLA Ops:
  1.3 0.0 copy-start
  1.3 1.2 %copy-done = bf16[1024,512]{1,0:T(8,128)(2,1)S(1)} copy-done((bf16[1024,512]{1,0:T(8,128)(2,1)S(1)}, bf16[1024,512]{1,0:T(8,128)(2,1)}, u32[]{:S(2)}) %copy-start) | copy-done | bytes 1048600
  2.5 0.0 copy-start.1
  2.5 1.2 %copy-done.1 = bf16[1,1024,512]{2,1,0:T(8,128)(2,1)S(1)} copy-done((bf16[1,1024,512]{2,1,0:T(8,128)(2,1)S(1)}, bf16[1,1024,512]{2,1,0:T(8,128)(2,1)}, u32[]{:S(2)}) %copy-start.1) | copy-done | bytes 1048600
  3.7 0.0 copy-start.2
  3.7 1.0 %copy-done.2 = bf16[1,512,512]{2,1,0:T(8,128)(2,1)S(1)} copy-done((bf16[1,512,512]{2,1,0:T(8,128)(2,1)S(1)}, bf16[1,512,512]{2,1,0:T(8,128)(2,1)}, u32[]{:S(2)}) %copy-start.2) | copy-done | bytes 524312
  4.8 0.0 copy-start.3
  4.8 1.0 %copy-done.3 = bf16[1,512,512]{2,1,0:T(8,128)(2,1)S(1)} copy-done((bf16[1,512,512]{2,1,0:T(8,128)(2,1)S(1)}, bf16[1,512,512]{2,1,0:T(8,128)(2,1)}, u32[]{:S(2)}) %copy-start.3) | copy-done | bytes 524312
  5.8 0.0 copy-start.4
  5.8 0.9 %copy-done.4 = bf16[256,512]{1,0:T(8,128)(2,1)S(1)} copy-done((bf16[256,512]{1,0:T(8,128)(2,1)S(1)}, bf16[256,512]{1,0:T(8,128)(2,1)}, u32[]{:S(2)}) %copy-start.4) | copy-done | bytes 262168
  6.8 75.5 %shard_map.93 = (bf16[256,512]{1,0:T(8,128)(2,1)S(1)}, bf16[1024,256]{1,0:T(8,128)(2,1)S(1)}, f32[32,512]{1,0:T(8,128)S(1)}, f32[32,512]{1,0:T(8,128)S(1)}) custom-call(bf16[1024,512]{1,0:T(8,128)(2,1)S(1)} %copy-done, bf16[256,512]{1,0:T(8,128)(2,1)S(1)} %copy-done.4, f32[1]{0:T(128)S(6)} %copy.14.scale_ref, bf16[1024,512]{1,0:T(8,128)(2,1)S(1)} %bitcast.5, ...), custom_call_target="tpu_custom_call" | custom-call | tf_op jit(solution)/shard_map/pallas_call | solution.py:682
  82.3 0.7 copy.15
  83.0 0.8 copy.16
  83.8 0.6 copy.17
  84.4 0.6 copy.18
Async XLA Ops:
  1.3 1.2 %copy-start = (bf16[1024,512]{1,0:T(8,128)(2,1)S(1)}, bf16[1024,512]{1,0:T(8,128)(2,1)}, u32[]{:S(2)}) copy-start(bf16[1024,512]{1,0:T(8,128)(2,1)} %text.1) | copy-start | bytes 3145732
  2.5 1.2 %copy-start.1 = (bf16[1,1024,512]{2,1,0:T(8,128)(2,1)S(1)}, bf16[1,1024,512]{2,1,0:T(8,128)(2,1)}, u32[]{:S(2)}) copy-start(bf16[1,1024,512]{2,1,0:T(8,128)(2,1)} %param.9) | copy-start | bytes 3145732
  3.7 1.0 %copy-start.2 = (bf16[1,512,512]{2,1,0:T(8,128)(2,1)S(1)}, bf16[1,512,512]{2,1,0:T(8,128)(2,1)}, u32[]{:S(2)}) copy-start(bf16[1,512,512]{2,1,0:T(8,128)(2,1)} %param.10) | copy-start | bytes 1572868
  4.8 1.0 %copy-start.3 = (bf16[1,512,512]{2,1,0:T(8,128)(2,1)S(1)}, bf16[1,512,512]{2,1,0:T(8,128)(2,1)}, u32[]{:S(2)}) copy-start(bf16[1,512,512]{2,1,0:T(8,128)(2,1)} %param.11) | copy-start | bytes 1572868
  5.8 0.9 %copy-start.4 = (bf16[256,512]{1,0:T(8,128)(2,1)S(1)}, bf16[256,512]{1,0:T(8,128)(2,1)}, u32[]{:S(2)}) copy-start(bf16[256,512]{1,0:T(8,128)(2,1)} %image.1) | copy-start | bytes 786436

commit v5 on v4

--- a/solution.py
+++ b/solution.py
@@ -41,21 +41,29 @@
     return pl.ds(pl.multiple_of(index * size, size), size)
 
 
+def leave(*refs):
+    copies = [pltpu.make_async_copy(refs[k], refs[4 + k], refs[8].at[k]) for k in range(4)]
+    for c in copies:
+        c.start()
+    for c in copies:
+        c.wait()
+
+
 def make_kernel(n_sec, n_dp, n_mp):
     chips = n_mp // CORES
     line = n_sec * chips
     n_el = n_sec * n_mp
 
     def kernel(
-        text, image, scale_ref, hidden, w_in, w_out,
+        text_hbm, image_hbm, scale_ref, hidden_hbm, w_in_hbm, w_out_hbm,
         image_out, input_out, first_out, second_out,
-        text_low, cols, scores, sgrad, row_max, row_sum, row_lse, col_lse, row_st, row_rx, col_st, col_rx,
+        text, image, hidden, text_low, cols, scores, sgrad, row_max, row_sum, row_lse, col_lse, row_st, row_rx, row_mix, col_st, col_rx,
         wi_all, wo_all, h_own, t_full, t_keep, t_sx, t_sr, t_tx, t_rx,
         g_st, g_all, slope_own, in_st, act_all, slope_all, pre_all,
         w_full, w_tx, w_rx, w_sum, w_st, w_end, i_tx, i_rx, i_own, i_st, i_end,
         gat_s, gat_r, cs_s, cs_r, rs_s, rs_r, ww_s, ww_r, h_s, h_r,
         ts_s, ts_r, tc_s, tc_r, gs_s, gs_r, gr_s, in_s, in_r, ir_s,
-        wc_s, wc_r, w_s, w_r, im_s, im_r, io_s, io_r,
+        ld_s, wc_s, wc_r, w_s, w_r, im_s, im_r, io_s, io_r,
     ):
         s = lax.axis_index("section")
         d = lax.axis_index("dp")
@@ -102,6 +110,8 @@
         def away(step):
             return (-step[0] % RING, -step[1] % RING)
 
+        hops = (2, 3, 1, 0) if line == 4 else tuple(range(line - 1, -1, -1))
+
         def others(mine, count):
             return [lax.rem(mine + k, count) for k in range(1, count)]
 
@@ -116,6 +126,15 @@
             sent.append(c)
 
         with jax.named_scope("a_barrier"):
+            loads = [
+                pltpu.make_async_copy(src, dst, ld_s.at[k])
+                for k, (src, dst) in enumerate((
+                    (image_hbm, image), (text_hbm, text), (hidden_hbm, hidden),
+                    (w_in_hbm, wi_all.at[e]), (w_out_hbm, wo_all.at[e]),
+                ))
+            ]
+            for load in loads:
+                load.start()
             barrier = pltpu.get_barrier_semaphore()
             for p in others(d, n_dp):
                 pl.semaphore_signal(barrier, inc=1, device_id={"dp": p}, device_id_type=MESH)
@@ -124,11 +143,9 @@
                     barrier, inc=1, device_id={"section": q // n_mp, "mp": lax.rem(q, n_mp)},
                     device_id_type=MESH,
                 )
+            loads[0].wait()
             own_unit, _ = unit_rows(image[tile(s, half), :])
             cols[0:half, :] = own_unit.astype(BF16)
-            h_own[s] = hidden[tile(e, chunk), :]
-            wi_all[e] = w_in[...]
-            wo_all[e] = w_out[...]
             pl.semaphore_wait(barrier, n_dp + n_el - 2)
 
         quarter = half // 4
@@ -162,8 +179,12 @@
         for way in ("Z-", "Z+"):
             forward((0, 0), "A", way)
 
+        for load in loads[2:]:
+            load.wait()
+        h_own[s] = hidden[tile(e, chunk), :]
         mate = (1 - s) * n_mp + m
         push(hidden.at[tile(mate, chunk), :], h_own.at[s], h_s, h_r, {"section": 1 - s})
+        w_in, w_out = wi_all.at[e], wo_all.at[e]
         ww = ((w_in, wi_all), (w_out, wo_all))
         z_at, y_at = d // RING, lax.rem(d, RING)
         cell = (z_at * RING + y_at, y_at * RING + z_at)
@@ -185,11 +206,12 @@
             push(ww[which][0].at[part, :], ww[which][1].at[e, part, :], ww_s.at[which, lane],
                  ww_r.at[which, n_el + lane], at(far(toward), core))
 
-        for part, lane in ((top, 0), (rest, 2)):
-            neighbour(0, line - 1, part, 1 + lane)
-            neighbour(1, 1, part, 2 + lane)
-        neighbour(1, line - 1, top, 1)
-        neighbour(0, 1, top, 2)
+        def both_ways(which):
+            for part, lane in ((top, 0), (rest, 2)):
+                neighbour(which, line - 1, part, 1 + lane)
+                neighbour(which, 1, part, 2 + lane)
+
+        both_ways(0)
 
         for which in (0, 1):
             push(ww[which][0], ww[which][1].at[e], ww_s.at[which, 0], ww_r.at[which, e],
@@ -232,10 +254,10 @@
             return 1.0 / (1.0 + jnp.exp(-GELU * pre))
 
         with jax.named_scope("b_pre"):
-            @pl.loop(0, line)
-            def _(r):
-                unit, _ = unit_rows(text[tile(r, pair), :])
-                text_low[tile(r, pair), :] = unit.astype(BF16)
+            loads[1].wait()
+            for i, hop in enumerate(hops):
+                unit, _ = unit_rows(text[tile(far(hop), pair), :])
+                text_low[i * pair : (i + 1) * pair, :] = unit.astype(BF16)
 
             @pl.loop(0, line)
             def _(r):
@@ -244,37 +266,44 @@
                 act_all[tile(r, pair), :] = (pre * sigm).astype(BF16)
                 slope_all[tile(r, pair), :] = sigm + GELU * pre * sigm * (1.0 - sigm)
 
-        def pair_scores(one, two, fresh):
-            piece = jnp.concatenate(
-                [cols[slot(k) * half : (slot(k) + 1) * half, :] for k in (one, two)], axis=0)
+        def group_scores(*group, fresh=False):
+            piece = [cols[slot(k) * half : (slot(k) + 1) * half, :] for k in group]
+            piece = piece[0] if len(piece) == 1 else jnp.concatenate(piece, axis=0)
             peak = total = None
             for r in range(line):
                 part = pl.ds(r * pair, pair)
                 value = mult2 * dot_nt(text_low[part, :], piece)
-                left, right = value[:, 0:half], value[:, half : 2 * half]
-                scores[slot(one), part, :] = left
-                scores[slot(two), part, :] = right
-                best = jnp.maximum(left, right)
+                blocks = [value[:, k * half : (k + 1) * half] for k in range(len(group))]
+                for k, block in zip(group, blocks):
+                    scores[slot(k), part, :] = block
+                best = blocks[0]
+                for block in blocks[1:]:
+                    best = jnp.maximum(best, block)
                 if not fresh:
                     best = jnp.maximum(best, row_max[part, :])
-                mass = jnp.exp2(left - best) + jnp.exp2(right - best)
-                if not fresh:
-                    mass = mass + row_sum[part, :] * jnp.exp2(row_max[part, :] - best)
+                    mass = row_sum[part, :] * jnp.exp2(row_max[part, :] - best)
+                    for block in blocks:
+                        mass = mass + jnp.exp2(block - best)
+                    row_sum[part, :] = mass
+                else:
+                    row_sum[part, :] = jnp.ones(best.shape, F32)
                 row_max[part, :] = best
-                row_sum[part, :] = mass
-                top = jnp.max(value, axis=0, keepdims=True)
+                high = jnp.max(value, axis=0, keepdims=True)
                 if peak is None:
-                    peak = top
+                    peak = high
                     total = jnp.sum(jnp.exp2(value - peak), axis=0, keepdims=True)
                 else:
-                    top = jnp.maximum(peak, top)
-                    total = total * jnp.exp2(peak - top) + jnp.sum(
-                        jnp.exp2(value - top), axis=0, keepdims=True)
-                    peak = top
-            for k, step in enumerate((one, two)):
+                    high = jnp.maximum(peak, high)
+                    total = total * jnp.exp2(peak - high) + jnp.sum(
+                        jnp.exp2(value - high), axis=0, keepdims=True)
+                    peak = high
+            for k, step in enumerate(group):
                 p = shift(step)
                 col_st[pl.ds(p, 1), :] = peak[:, k * half : (k + 1) * half]
                 col_st[pl.ds(n_dp + p, 1), :] = total[:, k * half : (k + 1) * half]
+
+        with jax.named_scope("c_own"):
+            group_scores((0, 0), fresh=True)
 
         with jax.named_scope("c_blocks"):
             landed((0, 1), "A")
@@ -297,14 +326,14 @@
             forward((0, 3), "B1", "Y+")
             landed((3, 0), "A")
             forward((3, 0), "A1", "Z+")
-            pair_scores((0, 0), (0, 1), True)
-            for name, way in (("A0", "Y-"), ("A1", "Y+")):
+            group_scores((0, 1), (0, 3))
+            group_scores((1, 0), (3, 0))
+            for name in ("A0", "A1"):
                 landed((0, 2), name)
                 forward((0, 2), name, "Z-", "Z+")
             for name in ("B0", "B1"):
                 landed((2, 0), name)
                 forward((2, 0), name, "Y-", "Y+")
-            pair_scores((0, 3), (1, 0), False)
             for dy in (1, 3):
                 landed((1, dy), "A")
                 forward((1, dy), "A0", "Z-")
@@ -315,9 +344,9 @@
                 forward((dz, 1), "B0", "Y-")
                 landed((dz, 3), "B")
                 forward((dz, 3), "B1", "Y+")
-            pair_scores((3, 0), (1, 1), False)
             cross_first(0)
             cross_first(1)
+            group_scores((1, 1), (1, 3))
             for name in ("A0", "A1"):
                 landed((1, 2), name)
                 landed((3, 2), name)
@@ -328,25 +357,23 @@
                 landed((2, 3), name)
             forward((2, 1), "B0", "Y-")
             forward((2, 3), "B1", "Y+")
-            pair_scores((1, 3), (3, 1), False)
+            group_scores((3, 1), (3, 3))
             for name in ("B0", "B1"):
                 landed((0, 2), name)
             for name in ("A0", "A1"):
                 landed((2, 0), name)
-            pair_scores((3, 3), (0, 2), False)
+            group_scores((0, 2), (2, 0))
             for name in ("B0", "B1"):
                 landed((1, 2), name)
-            pair_scores((2, 0), (1, 2), False)
-            for name in ("B0", "B1"):
                 landed((3, 2), name)
+            group_scores((1, 2), (3, 2))
             for name in ("A0", "A1"):
                 landed((2, 1), name)
-            pair_scores((3, 2), (2, 1), False)
-            for name in ("A0", "A1"):
                 landed((2, 3), name)
+            group_scores((2, 1), (2, 3))
             for name in ("A0", "A1", "B0", "B1"):
                 landed((2, 2), name)
-            pair_scores((2, 3), (2, 2), False)
+            group_scores((2, 2))
 
         with jax.named_scope("d_colsend"):
             col_rx[d] = col_st[...]
@@ -356,17 +383,17 @@
         with jax.named_scope("e_rowstat"):
             for r in range(n_el):
                 part = pl.ds(r * chunk, chunk)
+                place = far(hops[r // CORES]) * CORES + r % CORES
                 peak = jnp.max(row_max[part, :], axis=1, keepdims=True)
                 acc = jnp.sum(row_sum[part, :] * jnp.exp2(row_max[part, :] - peak), axis=1,
                               keepdims=True)
-                row_st[r : r + 1, :] = jnp.broadcast_to(peak, (chunk, LANES)).T[0:1, :]
-                row_st[n_el + r : n_el + r + 1, :] = jnp.broadcast_to(acc, (chunk, LANES)).T[0:1, :]
+                row_st[pl.ds(place, 1), :] = jnp.broadcast_to(peak, (chunk, LANES)).T[0:1, :]
+                row_st[pl.ds(n_el + place, 1), :] = jnp.broadcast_to(acc, (chunk, LANES)).T[0:1, :]
             row_rx[e] = row_st[...]
             for q in others(e, n_el):
                 push(row_st, row_rx.at[e], rs_s.at[q], rs_r.at[e],
                      {"section": q // n_mp, "mp": lax.rem(q, n_mp)})
-            neighbour(1, line - 1, rest, 3)
-            neighbour(0, 1, rest, 4)
+            both_ways(1)
 
         def merge(rx, count, n):
             peak = rx[0, 0:n, :]
@@ -377,9 +404,23 @@
                 acc = acc + rx[k, n : 2 * n, :] * jnp.exp2(rx[k, 0:n, :] - peak)
             return peak + (jnp.log(acc) * LOG2E + 1.0)
 
+        def slopes(index):
+            pre = dot_nn(h_own[index // n_mp], wi_all[index])
+            sigm = sigmoid(pre)
+            slope_own[index] = sigm + GELU * pre * sigm * (1.0 - sigm)
+
         with jax.named_scope("f_cross"):
             cross_second(0)
             cross_second(1)
+            relay_weight(0, 1)
+            relay_weight(0, line - 1)
+            arrived(h_own.at[1 - s], h_r)
+            for step in (0, 1, line - 1):
+                slopes(far(step) * CORES + core)
+            for step in (0, 1, line - 1):
+                index = far(step) * CORES + sib
+                arrived(wi_all.at[index], ww_r.at[0, index])
+                slopes(index)
 
         with jax.named_scope("f_merge"):
             for p in sources(d, n_dp):
@@ -387,45 +428,43 @@
             col_lse[...] = merge(col_rx, n_dp, n_dp)
             for q in sources(e, n_el):
                 arrived(row_rx.at[q], rs_r.at[q])
-            merged = merge(row_rx, n_el, n_el)
+            row_mix[...] = merge(row_rx, n_el, n_el)
             for r in range(n_el):
+                place = far(hops[r // CORES]) * CORES + r % CORES
                 row_lse[r * chunk : (r + 1) * chunk, :] = jnp.broadcast_to(
-                    merged[r : r + 1, :], (LANES, chunk)).T
-
-        def score_rows(r):
-            base = row_lse[tile(r, pair), :]
+                    row_mix[pl.ds(place, 1), :], (LANES, chunk)).T
+
+        def score_rows(i):
+            part = slice(i * pair, (i + 1) * pair)
+            base = row_lse[part, :]
+            offset = (m - far(hops[i])) * pair + s * half
             for step in steps:
                 k = slot(step)
-                value = scores[k, tile(r, pair), :]
+                value = scores[k, part, :]
                 low = col_lse[pl.ds(shift(step), 1), :]
                 both = jnp.exp2(value - base) + jnp.exp2(value - low)
-                sgrad[tile(r, pair), k * half : (k + 1) * half] = both.astype(BF16)
-
-            @pl.when(r == m)
-            def _():
-                line_at = tile(m * n_sec + s, half)
-                value = scores[0, line_at, :]
-                both = jnp.exp2(value - row_lse[line_at, :]) + jnp.exp2(
-                    value - col_lse[pl.ds(d, 1), :])
-                diagonal = lax.broadcasted_iota(jnp.int32, (half, half), 0) == (
-                    lax.broadcasted_iota(jnp.int32, (half, half), 1))
-                sgrad[line_at, 0:half] = (both - jnp.where(diagonal, 1.0, 0.0)).astype(BF16)
+                if k == 0:
+                    diagonal = lax.broadcasted_iota(jnp.int32, (pair, half), 0) == (
+                        lax.broadcasted_iota(jnp.int32, (pair, half), 1) + offset)
+                    both = both - jnp.where(diagonal, 1.0, 0.0)
+                sgrad[part, k * half : (k + 1) * half] = both.astype(BF16)
 
         def join(where):
             arrived(t_sr.at[where], ts_r.at[where])
             return t_keep[where] + t_sr[where].astype(F32)
 
-        hops = (2, 3, 1, 0) if line == 4 else tuple(range(line - 1, -1, -1))
 
         def t_send(where, slot):
             return copy(t_tx.at[where], t_rx.at[spot], tc_s.at[slot], tc_r.at[spot],
                         at(where, core))
 
         with jax.named_scope("g_scorerows"):
+            score_rows(0)
             for i, hop in enumerate(hops):
                 where = far(hop)
-                score_rows(where)
-                t_full[...] = dot_nn(sgrad[tile(where, pair), :], cols[...])
+                t_full[...] = dot_nn(sgrad[i * pair : (i + 1) * pair, :], cols[...])
+                if i + 1 < line:
+                    score_rows(i + 1)
                 t_sx[where] = t_full[tile(sib, chunk), :].astype(BF16)
                 push(t_sx.at[where], t_sr.at[where], ts_s.at[i], ts_r.at[where], at(spot, sib))
                 t_keep[where] = t_full[tile(core, chunk), :]
@@ -436,9 +475,8 @@
                          at(last, core))
 
         with jax.named_scope("g_relay"):
-            for which in (0, 1):
-                relay_weight(which, 1)
-                relay_weight(which, line - 1)
+            relay_weight(1, 1)
+            relay_weight(1, line - 1)
 
         fold = half // 2
 
@@ -485,20 +523,14 @@
             cross_third(0)
             cross_third(1)
 
-        def slopes(layer):
-            for j in range(n_mp):
-                pre = dot_nn(h_own[layer], wi_all[layer * n_mp + j])
-                sigm = sigmoid(pre)
-                slope_own[layer, j] = sigm + GELU * pre * sigm * (1.0 - sigm)
-
         with jax.named_scope("j_weights"):
-            arrived(h_own.at[1 - s], h_r)
+            slopes(cross)
+            index = far(2) * CORES + sib
+            arrived(wi_all.at[index], ww_r.at[0, index])
+            slopes(index)
             for step in range(line):
                 index = far(step) * CORES + sib
-                for which in (0, 1):
-                    arrived(ww[which][1].at[index], ww_r.at[which, index])
-            for layer in range(n_sec):
-                slopes(layer)
+                arrived(wo_all.at[index], ww_r.at[1, index])
 
         with jax.named_scope("i_topgrad"):
             total = join(spot)
@@ -544,7 +576,7 @@
             for j in range(n_mp):
                 index = layer * n_mp + j
                 back = dot_nt(g_st[layer], wo_all[index])
-                grad = (back * slope_own[layer, j]).astype(BF16)
+                grad = (back * slope_own[index]).astype(BF16)
                 total = total + dot_nt(grad, wi_all[index])
             if layer > 0:
                 g_st[layer - 1] = total.astype(BF16)
@@ -579,7 +611,6 @@
                 push(g_all.at[index], g_all.at[index], gr_s.at[hop], gs_r.at[index],
                      at(spot, sib))
                 weight_rows(index)
-            image_second()
             for hop in (0, 1, 3, 2) if line == 4 else range(line):
                 index = far(hop) * CORES + sib
                 arrived(g_all.at[index], gs_r.at[index])
@@ -630,6 +661,13 @@
                 arrived(slab(index), in_r.at[index])
                 push(slab(index), slab(index), ir_s.at[hop], in_r.at[index], at(spot, sib))
 
+        with jax.named_scope("p_isecond"):
+            image_second()
+
+        with jax.named_scope("p_wsecond"):
+            weight_second(1)
+            weight_second(0)
+
         with jax.named_scope("q_image"):
             image_half = tile(s, half)
             unit, length = unit_rows(image[image_half, :])
@@ -644,10 +682,6 @@
             push(image_out.at[image_half, :], image_out.at[image_half, :], io_s, io_r,
                  {"section": 1 - s})
 
-        with jax.named_scope("p_wsecond"):
-            weight_second(1)
-            weight_second(0)
-
         with jax.named_scope("q_wsum"):
             weight_last(1, second_out)
             weight_last(0, first_out)
@@ -679,17 +713,21 @@
         chunk = rows // n_el
         dma = pltpu.SemaphoreType.DMA
         vmem = pl.BlockSpec(memory_space=pltpu.VMEM)
+        hbm = pl.BlockSpec(memory_space=pltpu.HBM)
         out = pl.pallas_call(
             make_kernel(n_sec, n_dp, n_mp),
             out_shape=(
-                jax.ShapeDtypeStruct((own, feats), BF16),
-                jax.ShapeDtypeStruct((rows, feats // n_sec), BF16),
-                jax.ShapeDtypeStruct((share, hid), F32),
-                jax.ShapeDtypeStruct((share, hid), F32),
+                pltpu.VMEM((own, feats), BF16),
+                pltpu.VMEM((rows, feats // n_sec), BF16),
+                pltpu.VMEM((share, hid), F32),
+                pltpu.VMEM((share, hid), F32),
             ),
-            in_specs=[vmem, vmem, pl.BlockSpec(memory_space=pltpu.SMEM), vmem, vmem, vmem],
+            in_specs=[hbm, hbm, pl.BlockSpec(memory_space=pltpu.SMEM), hbm, hbm, hbm],
             out_specs=(vmem,) * 4,
             scratch_shapes=[
+                pltpu.VMEM((rows, feats), BF16),
+                pltpu.VMEM((own, feats), BF16),
+                pltpu.VMEM((rows, feats), BF16),
                 pltpu.VMEM((rows, feats), BF16),
                 pltpu.VMEM((columns, feats), BF16),
                 pltpu.VMEM((n_dp, rows, half), F32),
@@ -700,6 +738,7 @@
                 pltpu.VMEM((n_dp, half), F32),
                 pltpu.VMEM((2 * n_el, chunk), F32),
                 pltpu.VMEM((n_el, 2 * n_el, chunk), F32),
+                pltpu.VMEM((n_el, chunk), F32),
                 pltpu.VMEM((2 * n_dp, half), F32),
                 pltpu.VMEM((n_dp, 2 * n_dp, half), F32),
                 pltpu.VMEM((n_el, feats, hid), BF16),
@@ -713,7 +752,7 @@
                 pltpu.VMEM((line, chunk, feats), BF16),
                 pltpu.VMEM((n_sec, chunk, feats), BF16),
                 pltpu.VMEM((n_el, chunk, feats), BF16),
-                pltpu.VMEM((n_sec, n_mp, chunk, hid), F32),
+                pltpu.VMEM((n_el, chunk, hid), F32),
                 pltpu.VMEM((n_sec, chunk, feats // n_sec), BF16),
                 pltpu.VMEM((rows, hid), BF16),
                 pltpu.VMEM((rows, hid), F32),
@@ -740,16 +779,24 @@
                 dma((line,)),
                 dma((line,)), dma((n_el,)),
                 dma((line,)),
+                dma((5,)),
                 dma((2, 2 * RING)), dma((2, 2 * RING)),
                 dma((2, 2 * RING)), dma((2, 2 * RING)),
                 dma((2, 2 * RING)), dma((2, 2 * RING)),
                 dma, dma,
             ],
             compiler_params=pltpu.CompilerParams(
-                collective_id=0, has_side_effects=True, vmem_limit_bytes=52000000
+                collective_id=0, has_side_effects=True, vmem_limit_bytes=57000000
             ),
         )(text, image, scale, hidden[0], w_in[0], w_out[0])
-        image_grad, input_grad, first, second = out
+        image_grad, input_grad, first, second = pl.pallas_call(
+            leave,
+            out_shape=tuple(jax.ShapeDtypeStruct(x.shape, x.dtype) for x in out),
+            in_specs=[vmem] * 4,
+            out_specs=(hbm,) * 4,
+            scratch_shapes=[dma((4,))],
+            compiler_params=pltpu.CompilerParams(vmem_limit_bytes=4000000),
+        )(*out)
         return (image_grad, input_grad, first[None], second[None])
 
     return jax.shard_map(

time: 85.3 us -> 80.3 us (0.941); the launches traced: 85 us -> 79 us
  local copies, waits for them, and re-layouts: 8.23 us -> 0 us
  Pallas kernels: 75.5 us -> 77.5 us
    unnamed x14 -> x0, local copies, waits for them, and re-layouts: 8.23 us -> none
    pallas_call x1 -> x2, Pallas kernels: 75.5 us -> 77.5 us  [the longest x1 76.6 us: body(): pl.pallas_call(make_kernel(n_sec, n_dp, n_mp), out_shape=(pltpu.VMEM((own...]
where the time goes in v5:
time: 80.3 us; the launch traced here: 79 us
  Pallas kernels  77.5 us (97%)
  between operations  1.45 us (2%)
    pallas_call x1, Pallas kernels, body(): pl.pallas_call(make_kernel(n_sec, n_dp, n_mp), out_shape=(pltpu.VMEM((own...  76.6 us

profile of v5, /device:TPU:0, one launch (start us, length us, event | category | flops | bytes accessed | tf_op | source)
XLA Modules:
  0.0 79.0 jit_solution(15598873738057134408)
XLA Ops:
  1.3 76.6 %shard_map.93 = (bf16[256,512]{1,0:T(8,128)(2,1)S(1)}, bf16[1024,256]{1,0:T(8,128)(2,1)S(1)}, f32[32,512]{1,0:T(8,128)S(1)}, f32[32,512]{1,0:T(8,128)S(1)}) custom-call(bf16[1024,512]{1,0:T(8,128)(2,1)} %text_hbm.1, bf16[256,512]{1,0:T(8,128)(2,1)} %image_hbm.1, f32[1]{0:T(128)S(6)} %copy.10.scale_ref, bf16[1024,512]{1,0:T(8,128)(2,1)} %bitcast.5, ...), custom_call_target="tpu_custom_call" | custom-call | tf_op jit(solution)/shard_map/pallas_call | solution.py:717
  77.9 0.9 %shard_map.94 = (bf16[256,512]{1,0:T(8,128)(2,1)}, bf16[1024,256]{1,0:T(8,128)(2,1)}, f32[32,512]{1,0:T(8,128)}, f32[32,512]{1,0:T(8,128)}) custom-call(bf16[256,512]{1,0:T(8,128)(2,1)S(1)} %get-tuple-element.12.refs_0_, bf16[1024,256]{1,0:T(8,128)(2,1)S(1)} %get-tuple-element.13.refs_1_, f32[32,512]{1,0:T(8,128)S(1)} %get-tuple-element.14.refs_2_, ...), custom_call_target="tpu_custom_call" | custom-call | tf_op jit(solution)/shard_map/pallas_call | solution.py:792

commit v6 on v5

--- a/solution.py
+++ b/solution.py
@@ -206,12 +206,13 @@
             push(ww[which][0].at[part, :], ww[which][1].at[e, part, :], ww_s.at[which, lane],
                  ww_r.at[which, n_el + lane], at(far(toward), core))
 
-        def both_ways(which):
-            for part, lane in ((top, 0), (rest, 2)):
+        def both_ways(which, *parts):
+            for part, lane in parts:
                 neighbour(which, line - 1, part, 1 + lane)
                 neighbour(which, 1, part, 2 + lane)
 
-        both_ways(0)
+        both_ways(0, (top, 0), (rest, 2))
+        both_ways(1, (top, 0))
 
         for which in (0, 1):
             push(ww[which][0], ww[which][1].at[e], ww_s.at[which, 0], ww_r.at[which, e],
@@ -297,10 +298,10 @@
                     total = total * jnp.exp2(peak - high) + jnp.sum(
                         jnp.exp2(value - high), axis=0, keepdims=True)
                     peak = high
+            level = peak + jnp.log(total) * LOG2E
             for k, step in enumerate(group):
                 p = shift(step)
-                col_st[pl.ds(p, 1), :] = peak[:, k * half : (k + 1) * half]
-                col_st[pl.ds(n_dp + p, 1), :] = total[:, k * half : (k + 1) * half]
+                col_st[pl.ds(p, 1), :] = level[:, k * half : (k + 1) * half]
 
         with jax.named_scope("c_own"):
             group_scores((0, 0), fresh=True)
@@ -347,6 +348,12 @@
             cross_first(0)
             cross_first(1)
             group_scores((1, 1), (1, 3))
+            group_scores((3, 1), (3, 3))
+            for name in ("B0", "B1"):
+                landed((0, 2), name)
+            for name in ("A0", "A1"):
+                landed((2, 0), name)
+            group_scores((0, 2), (2, 0))
             for name in ("A0", "A1"):
                 landed((1, 2), name)
                 landed((3, 2), name)
@@ -357,12 +364,6 @@
                 landed((2, 3), name)
             forward((2, 1), "B0", "Y-")
             forward((2, 3), "B1", "Y+")
-            group_scores((3, 1), (3, 3))
-            for name in ("B0", "B1"):
-                landed((0, 2), name)
-            for name in ("A0", "A1"):
-                landed((2, 0), name)
-            group_scores((0, 2), (2, 0))
             for name in ("B0", "B1"):
                 landed((1, 2), name)
                 landed((3, 2), name)
@@ -387,21 +388,21 @@
                 peak = jnp.max(row_max[part, :], axis=1, keepdims=True)
                 acc = jnp.sum(row_sum[part, :] * jnp.exp2(row_max[part, :] - peak), axis=1,
                               keepdims=True)
-                row_st[pl.ds(place, 1), :] = jnp.broadcast_to(peak, (chunk, LANES)).T[0:1, :]
-                row_st[pl.ds(n_el + place, 1), :] = jnp.broadcast_to(acc, (chunk, LANES)).T[0:1, :]
+                level = peak + jnp.log(acc) * LOG2E
+                row_st[pl.ds(place, 1), :] = jnp.broadcast_to(level, (chunk, LANES)).T[0:1, :]
             row_rx[e] = row_st[...]
             for q in others(e, n_el):
                 push(row_st, row_rx.at[e], rs_s.at[q], rs_r.at[e],
                      {"section": q // n_mp, "mp": lax.rem(q, n_mp)})
-            both_ways(1)
-
-        def merge(rx, count, n):
-            peak = rx[0, 0:n, :]
+            both_ways(1, (rest, 2))
+
+        def merge(rx, count):
+            peak = rx[0]
             for k in range(1, count):
-                peak = jnp.maximum(peak, rx[k, 0:n, :])
+                peak = jnp.maximum(peak, rx[k])
             acc = jnp.zeros(peak.shape, F32)
             for k in range(count):
-                acc = acc + rx[k, n : 2 * n, :] * jnp.exp2(rx[k, 0:n, :] - peak)
+                acc = acc + jnp.exp2(rx[k] - peak)
             return peak + (jnp.log(acc) * LOG2E + 1.0)
 
         def slopes(index):
@@ -425,10 +426,10 @@
         with jax.named_scope("f_merge"):
             for p in sources(d, n_dp):
                 arrived(col_rx.at[p], cs_r.at[p])
-            col_lse[...] = merge(col_rx, n_dp, n_dp)
+            col_lse[...] = merge(col_rx, n_dp)
             for q in sources(e, n_el):
                 arrived(row_rx.at[q], rs_r.at[q])
-            row_mix[...] = merge(row_rx, n_el, n_el)
+            row_mix[...] = merge(row_rx, n_el)
             for r in range(n_el):
                 place = far(hops[r // CORES]) * CORES + r % CORES
                 row_lse[r * chunk : (r + 1) * chunk, :] = jnp.broadcast_to(
@@ -475,6 +476,8 @@
                          at(last, core))
 
         with jax.named_scope("g_relay"):
+            cross_third(0)
+            cross_third(1)
             relay_weight(1, 1)
             relay_weight(1, line - 1)
 
@@ -519,10 +522,6 @@
 
         mine = tile(e, chunk)
 
-        with jax.named_scope("h_cross"):
-            cross_third(0)
-            cross_third(1)
-
         with jax.named_scope("j_weights"):
             slopes(cross)
             index = far(2) * CORES + sib
@@ -591,14 +590,6 @@
             for layer in range(n_sec - 1, -1, -1):
                 feed_forward(layer)
 
-        with jax.named_scope("l_inspread"):
-            input_out[mine, :] = in_st[s]
-            push(in_st.at[s], slab(e), in_s.at[0], in_r.at[e], at(spot, sib))
-            for hop in hops[:-1]:
-                where = far(hop)
-                push(in_st.at[where // chips], slab(e), in_s.at[hop], in_r.at[e],
-                     at(where, core))
-
         def weight_rows(k):
             back = dot_nt(g_all[k], w_out[...])
             pre_all[tile(k, chunk), :] = (back * slope_all[tile(k, chunk), :]).astype(BF16)
@@ -611,6 +602,13 @@
                 push(g_all.at[index], g_all.at[index], gr_s.at[hop], gs_r.at[index],
                      at(spot, sib))
                 weight_rows(index)
+            input_out[mine, :] = in_st[s]
+            push(in_st.at[s], slab(e), in_s.at[0], in_r.at[e], at(spot, sib))
+            for hop in hops[:-1]:
+                where = far(hop)
+                push(in_st.at[where // chips], slab(e), in_s.at[hop], in_r.at[e],
+                     at(where, core))
+            image_second()
             for hop in (0, 1, 3, 2) if line == 4 else range(line):
                 index = far(hop) * CORES + sib
                 arrived(g_all.at[index], gs_r.at[index])
@@ -655,19 +653,6 @@
             w_tx[0] = grad.astype(BF16)
             send_weights(0)
 
-        with jax.named_scope("o_inrelay"):
-            for hop in hops[:-1]:
-                index = far(hop) * CORES + core
-                arrived(slab(index), in_r.at[index])
-                push(slab(index), slab(index), ir_s.at[hop], in_r.at[index], at(spot, sib))
-
-        with jax.named_scope("p_isecond"):
-            image_second()
-
-        with jax.named_scope("p_wsecond"):
-            weight_second(1)
-            weight_second(0)
-
         with jax.named_scope("q_image"):
             image_half = tile(s, half)
             unit, length = unit_rows(image[image_half, :])
@@ -681,6 +666,16 @@
                     unit[part, :], length[part, :], mult * total).astype(BF16)
             push(image_out.at[image_half, :], image_out.at[image_half, :], io_s, io_r,
                  {"section": 1 - s})
+
+        with jax.named_scope("o_inrelay"):
+            for hop in hops[:-1]:
+                index = far(hop) * CORES + core
+                arrived(slab(index), in_r.at[index])
+                push(slab(index), slab(index), ir_s.at[hop], in_r.at[index], at(spot, sib))
+
+        with jax.named_scope("p_wsecond"):
+            weight_second(1)
+            weight_second(0)
 
         with jax.named_scope("q_wsum"):
             weight_last(1, second_out)
@@ -736,11 +731,11 @@
                 pltpu.VMEM((rows, LANES), F32),
                 pltpu.VMEM((rows, LANES), F32),
                 pltpu.VMEM((n_dp, half), F32),
-                pltpu.VMEM((2 * n_el, chunk), F32),
-                pltpu.VMEM((n_el, 2 * n_el, chunk), F32),
                 pltpu.VMEM((n_el, chunk), F32),
-                pltpu.VMEM((2 * n_dp, half), F32),
-                pltpu.VMEM((n_dp, 2 * n_dp, half), F32),
+                pltpu.VMEM((n_el, n_el, chunk), F32),
+                pltpu.VMEM((n_el, chunk), F32),
+                pltpu.VMEM((n_dp, half), F32),
+                pltpu.VMEM((n_dp, n_dp, half), F32),
                 pltpu.VMEM((n_el, feats, hid), BF16),
                 pltpu.VMEM((n_el, hid, feats), BF16),
                 pltpu.VMEM((n_sec, chunk, feats), BF16),

time: 80.3 us -> 74.4 us (0.927); the launches traced: 79 us -> 74.3 us
  Pallas kernels: 77.5 us -> 72.9 us
    pallas_call x1, Pallas kernels: 76.6 us -> 71.9 us  [body(): pl.pallas_call(make_kernel(n_sec, n_dp, n_mp), out_shape=(pltpu.VMEM((own...]
where the time goes in v6:
time: 74.4 us; the launch traced here: 74.3 us
  Pallas kernels  72.9 us (98%)
  between operations  1.45 us (2%)
    pallas_call x1, Pallas kernels, body(): pl.pallas_call(make_kernel(n_sec, n_dp, n_mp), out_shape=(pltpu.VMEM((own...  71.9 us

profile of v6, /device:TPU:0, one launch (start us, length us, event | category | flops | bytes accessed | tf_op | source)
XLA Modules:
  0.0 74.3 jit_solution(7660995793873971075)
XLA Ops:
  1.3 71.9 %shard_map.93 = (bf16[256,512]{1,0:T(8,128)(2,1)S(1)}, bf16[1024,256]{1,0:T(8,128)(2,1)S(1)}, f32[32,512]{1,0:T(8,128)S(1)}, f32[32,512]{1,0:T(8,128)S(1)}) custom-call(bf16[1024,512]{1,0:T(8,128)(2,1)} %text_hbm.1, bf16[256,512]{1,0:T(8,128)(2,1)} %image_hbm.1, f32[1]{0:T(128)S(6)} %copy.10.scale_ref, bf16[1024,512]{1,0:T(8,128)(2,1)} %bitcast.5, ...), custom_call_target="tpu_custom_call" | custom-call | tf_op jit(solution)/shard_map/pallas_call | solution.py:712
  73.2 0.9 %shard_map.94 = (bf16[256,512]{1,0:T(8,128)(2,1)}, bf16[1024,256]{1,0:T(8,128)(2,1)}, f32[32,512]{1,0:T(8,128)}, f32[32,512]{1,0:T(8,128)}) custom-call(bf16[256,512]{1,0:T(8,128)(2,1)S(1)} %get-tuple-element.12.refs_0_, bf16[1024,256]{1,0:T(8,128)(2,1)S(1)} %get-tuple-element.13.refs_1_, f32[32,512]{1,0:T(8,128)S(1)} %get-tuple-element.14.refs_2_, ...), custom_call_target="tpu_custom_call" | custom-call | tf_op jit(solution)/shard_map/pallas_call | solution.py:787

commit v7 on v6

--- a/solution.py
+++ b/solution.py
@@ -62,7 +62,7 @@
         g_st, g_all, slope_own, in_st, act_all, slope_all, pre_all,
         w_full, w_tx, w_rx, w_sum, w_st, w_end, i_tx, i_rx, i_own, i_st, i_end,
         gat_s, gat_r, cs_s, cs_r, rs_s, rs_r, ww_s, ww_r, h_s, h_r,
-        ts_s, ts_r, tc_s, tc_r, gs_s, gs_r, gr_s, in_s, in_r, ir_s,
+        ts_s, ts_r, tc_s, tc_r, gs_s, gs_r, in_s, in_r,
         ld_s, wc_s, wc_r, w_s, w_r, im_s, im_r, io_s, io_r,
     ):
         s = lax.axis_index("section")
@@ -118,12 +118,11 @@
         def sources(mine, count):
             return [lax.rem(mine + count - k, count) for k in range(1, count)]
 
-        sent = []
-
         def push(*args):
-            c = copy(*args)
-            c.start()
-            sent.append(c)
+            copy(*args).start()
+
+        def left(ref, send):
+            copy(ref, ref, send, h_r, at(spot, sib)).wait_send()
 
         with jax.named_scope("a_barrier"):
             loads = [
@@ -136,8 +135,9 @@
             for load in loads:
                 load.start()
             barrier = pltpu.get_barrier_semaphore()
-            for p in others(d, n_dp):
-                pl.semaphore_signal(barrier, inc=1, device_id={"dp": p}, device_id_type=MESH)
+            for near in ((0, 1), (0, -1), (1, 0), (-1, 0)):
+                pl.semaphore_signal(
+                    barrier, inc=1, device_id={"dp": shift(near)}, device_id_type=MESH)
             for q in others(e, n_el):
                 pl.semaphore_signal(
                     barrier, inc=1, device_id={"section": q // n_mp, "mp": lax.rem(q, n_mp)},
@@ -146,12 +146,32 @@
             loads[0].wait()
             own_unit, _ = unit_rows(image[tile(s, half), :])
             cols[0:half, :] = own_unit.astype(BF16)
-            pl.semaphore_wait(barrier, n_dp + n_el - 2)
+            pl.semaphore_wait(barrier, n_el + 3)
 
         quarter = half // 4
         spans = {"A": (0, 2), "B": (2, 2), "A0": (0, 1), "A1": (1, 1), "B0": (2, 1), "B1": (3, 1)}
         ahead = {"Y-": (0, -1), "Y+": (0, 1), "Z-": (-1, 0), "Z+": (1, 0)}
-        passed = []
+        quads = {
+            "a": [((0, 2), "B0"), ((0, 2), "B1"), ((2, 0), "A0"), ((2, 0), "A1")],
+            "b": [(k, name) for k in ((1, 2), (3, 2)) for name in ("A0", "A1")]
+            + [(k, name) for k in ((2, 1), (2, 3)) for name in ("B0", "B1")],
+            "c": [(k, name) for k in ((1, 2), (3, 2)) for name in ("B0", "B1")],
+            "d": [(k, name) for k in ((2, 1), (2, 3)) for name in ("A0", "A1")],
+            "e": [((2, 2), name) for name in ("A0", "A1", "B0", "B1")],
+        }
+        ports = {}
+
+        def port(step, name):
+            key = (slot(step), name)
+            for group, members in quads.items():
+                if any(key == (slot(k), other) for k, other in members):
+                    key = group
+            return ports.setdefault(key, len(ports))
+
+        def landed_all(group):
+            count = len(quads[group])
+            k, name = quads[group][0]
+            arrived(cols.at[0 : count * quarter, :], gat_r.at[port(k, name)])
 
         def piece_of(step, name):
             first, count = spans[name]
@@ -162,13 +182,11 @@
             for way in directions:
                 move = ahead[way]
                 lands = (step[0] - move[0], step[1] - move[1])
-                c = copy(piece_of(step, name), piece_of(lands, name), gat_s.at[len(passed)],
-                         gat_r.at[slot(lands), spans[name][0]], {"dp": shift(move)})
-                c.start()
-                passed.append(c)
+                push(piece_of(step, name), piece_of(lands, name), gat_s,
+                     gat_r.at[port(lands, name)], {"dp": shift(move)})
 
         def landed(step, name):
-            arrived(piece_of(step, name), gat_r.at[slot(step), spans[name][0]])
+            arrived(piece_of(step, name), gat_r.at[port(step, name)])
 
         for way in ("Y-", "Y+"):
             forward((0, 0), "A", way)
@@ -197,59 +215,50 @@
 
         for which in (0, 1):
             part = tile(cell[which], bit)
-            push(ww[which][0].at[part, :], ww[which][1].at[e, part, :], wc_s.at[which, 0],
+            push(ww[which][0].at[part, :], ww[which][1].at[e, part, :], wc_s.at[which],
                  wc_r.at[which, 0], at(far(2), core))
         top = pl.ds(0, w_in.shape[0] // 2)
         rest = pl.ds(w_in.shape[0] // 2, w_in.shape[0] // 2)
 
-        def neighbour(which, toward, part, lane):
-            push(ww[which][0].at[part, :], ww[which][1].at[e, part, :], ww_s.at[which, lane],
-                 ww_r.at[which, n_el + lane], at(far(toward), core))
-
-        def both_ways(which, *parts):
-            for part, lane in parts:
-                neighbour(which, line - 1, part, 1 + lane)
-                neighbour(which, 1, part, 2 + lane)
-
-        both_ways(0, (top, 0), (rest, 2))
-        both_ways(1, (top, 0))
+        def neighbour(which, toward, part):
+            push(ww[which][0].at[part, :], ww[which][1].at[e, part, :], ww_s.at[which],
+                 ww_r.at[which, 1 if toward == 1 else 0], at(far(toward), core))
+
+        def both_ways(which):
+            for part in (top, rest):
+                neighbour(which, line - 1, part)
+                neighbour(which, 1, part)
+
+        both_ways(0)
 
         for which in (0, 1):
-            push(ww[which][0], ww[which][1].at[e], ww_s.at[which, 0], ww_r.at[which, e],
+            push(ww[which][0], ww[which][1].at[e], ww_s.at[which], ww_r.at[which, 2],
                  at(spot, sib))
 
         def cross_first(which):
             mine_bit = ww[which][1].at[cross, tile(cell[which], bit), :]
             arrived(mine_bit, wc_r.at[which, 0])
             for k in range(1, RING):
-                push(mine_bit, mine_bit, wc_s.at[which, k], wc_r.at[which, RING - k],
+                push(mine_bit, mine_bit, wc_s.at[which], wc_r.at[which, 1],
                      along(which, k))
 
         def cross_second(which):
-            for k in range(1, RING):
-                other = band[which] * RING + lax.rem(band[1 - which] + k, RING)
-                arrived(ww[which][1].at[cross, tile(other, bit), :], wc_r.at[which, k])
+            arrived(ww[which][1].at[cross, 0 : (RING - 1) * bit, :], wc_r.at[which, 1])
             group = ww[which][1].at[cross, tile(band[which], RING * bit), :]
             for k in range(1, RING):
-                push(group, group, wc_s.at[which, RING + k], wc_r.at[which, 2 * RING - k],
+                push(group, group, wc_s.at[which], wc_r.at[which, 2],
                      along(1 - which, k))
 
         def cross_third(which):
-            for k in range(1, RING):
-                other = lax.rem(band[which] + k, RING)
-                arrived(ww[which][1].at[cross, tile(other, RING * bit), :],
-                        wc_r.at[which, RING + k])
-            push(ww[which][1].at[cross], ww[which][1].at[cross], ww_s.at[which, 6],
-                 ww_r.at[which, cross], at(spot, sib))
+            arrived(ww[which][1].at[cross, 0 : (RING - 1) * RING * bit, :], wc_r.at[which, 2])
+            push(ww[which][1].at[cross], ww[which][1].at[cross], ww_s.at[which],
+                 ww_r.at[which, 2 if which else 3], at(spot, sib))
 
         def relay_weight(which, step):
             index = far(step) * CORES + core
             buf = ww[which][1].at[index]
-            for part, lane in ((top, 0), (rest, 2)):
-                arrived(ww[which][1].at[index, part, :],
-                        ww_r.at[which, n_el + lane + (1 if step == 1 else 2)])
-            push(buf, buf, ww_s.at[which, 5 if step == 1 else 7], ww_r.at[which, index],
-                 at(spot, sib))
+            arrived(buf, ww_r.at[which, 0 if step == 1 else 1])
+            push(buf, buf, ww_s.at[which], ww_r.at[which, 2], at(spot, sib))
 
         def sigmoid(pre):
             return 1.0 / (1.0 + jnp.exp(-GELU * pre))
@@ -349,37 +358,24 @@
             cross_first(1)
             group_scores((1, 1), (1, 3))
             group_scores((3, 1), (3, 3))
-            for name in ("B0", "B1"):
-                landed((0, 2), name)
-            for name in ("A0", "A1"):
-                landed((2, 0), name)
+            landed_all("a")
             group_scores((0, 2), (2, 0))
-            for name in ("A0", "A1"):
-                landed((1, 2), name)
-                landed((3, 2), name)
+            landed_all("b")
             forward((1, 2), "A0", "Z-")
             forward((3, 2), "A1", "Z+")
-            for name in ("B0", "B1"):
-                landed((2, 1), name)
-                landed((2, 3), name)
             forward((2, 1), "B0", "Y-")
             forward((2, 3), "B1", "Y+")
-            for name in ("B0", "B1"):
-                landed((1, 2), name)
-                landed((3, 2), name)
+            landed_all("c")
             group_scores((1, 2), (3, 2))
-            for name in ("A0", "A1"):
-                landed((2, 1), name)
-                landed((2, 3), name)
+            landed_all("d")
             group_scores((2, 1), (2, 3))
-            for name in ("A0", "A1", "B0", "B1"):
-                landed((2, 2), name)
+            landed_all("e")
             group_scores((2, 2))
 
         with jax.named_scope("d_colsend"):
             col_rx[d] = col_st[...]
             for p in others(d, n_dp):
-                push(col_st, col_rx.at[d], cs_s.at[p], cs_r.at[d], {"dp": p})
+                push(col_st, col_rx.at[d], cs_s, cs_r, {"dp": p})
 
         with jax.named_scope("e_rowstat"):
             for r in range(n_el):
@@ -392,9 +388,9 @@
                 row_st[pl.ds(place, 1), :] = jnp.broadcast_to(level, (chunk, LANES)).T[0:1, :]
             row_rx[e] = row_st[...]
             for q in others(e, n_el):
-                push(row_st, row_rx.at[e], rs_s.at[q], rs_r.at[e],
+                push(row_st, row_rx.at[e], rs_s, rs_r,
                      {"section": q // n_mp, "mp": lax.rem(q, n_mp)})
-            both_ways(1, (rest, 2))
+            both_ways(1)
 
         def merge(rx, count):
             peak = rx[0]
@@ -418,17 +414,14 @@
             arrived(h_own.at[1 - s], h_r)
             for step in (0, 1, line - 1):
                 slopes(far(step) * CORES + core)
+            arrived(wi_all.at[0:3], ww_r.at[0, 2])
             for step in (0, 1, line - 1):
-                index = far(step) * CORES + sib
-                arrived(wi_all.at[index], ww_r.at[0, index])
-                slopes(index)
+                slopes(far(step) * CORES + sib)
 
         with jax.named_scope("f_merge"):
-            for p in sources(d, n_dp):
-                arrived(col_rx.at[p], cs_r.at[p])
+            arrived(col_rx.at[0 : n_dp - 1], cs_r)
             col_lse[...] = merge(col_rx, n_dp)
-            for q in sources(e, n_el):
-                arrived(row_rx.at[q], rs_r.at[q])
+            arrived(row_rx.at[0 : n_el - 1], rs_r)
             row_mix[...] = merge(row_rx, n_el)
             for r in range(n_el):
                 place = far(hops[r // CORES]) * CORES + r % CORES
@@ -455,10 +448,6 @@
             return t_keep[where] + t_sr[where].astype(F32)
 
 
-        def t_send(where, slot):
-            return copy(t_tx.at[where], t_rx.at[spot], tc_s.at[slot], tc_r.at[spot],
-                        at(where, core))
-
         with jax.named_scope("g_scorerows"):
             score_rows(0)
             for i, hop in enumerate(hops):
@@ -467,47 +456,39 @@
                 if i + 1 < line:
                     score_rows(i + 1)
                 t_sx[where] = t_full[tile(sib, chunk), :].astype(BF16)
-                push(t_sx.at[where], t_sr.at[where], ts_s.at[i], ts_r.at[where], at(spot, sib))
+                push(t_sx.at[where], t_sr.at[where], ts_s, ts_r.at[where], at(spot, sib))
                 t_keep[where] = t_full[tile(core, chunk), :]
                 if i > 0:
                     last = far(hops[i - 1])
                     t_tx[last] = join(last).astype(BF16)
-                    push(t_tx.at[last], t_rx.at[spot], tc_s.at[i], tc_r.at[spot],
+                    push(t_tx.at[last], t_rx.at[spot - (spot > last).astype(jnp.int32)], tc_s, tc_r,
                          at(last, core))
 
         with jax.named_scope("g_relay"):
             cross_third(0)
             cross_third(1)
-            relay_weight(1, 1)
-            relay_weight(1, line - 1)
-
-        fold = half // 2
+
+        fold = feats // 2
 
         with jax.named_scope("h_image"):
             for g in (2, 1, 3, 0):
-                part = dot_tn(sgrad[:, g * RING * half : (g + 1) * RING * half], text_low[...])
-                for k in range(RING):
-                    low = part[k * half : k * half + fold, :]
-                    high = part[k * half + fold : (k + 1) * half, :]
-                    if g == 0:
-                        i_own[0, k] = low
-                    else:
-                        i_tx[0, g, k] = low.astype(BF16)
-                    if k == 0:
-                        i_own[1, g] = high
-                    else:
-                        i_tx[1, k, g] = high.astype(BF16)
-                if g > 0:
-                    push(i_tx.at[0, g], i_rx.at[0, RING - g], im_s.at[0, g], im_r.at[0, RING - g],
-                         along(1, g))
-            for k in (2, 1, 3):
-                push(i_tx.at[1, k], i_rx.at[1, RING - k], im_s.at[1, k], im_r.at[1, RING - k],
-                     along(0, k))
+                for which in (0, 1):
+                    ends = [(g, k) if which == 0 else (k, g) for k in range(RING)]
+                    block = jnp.concatenate(
+                        [sgrad[:, slot(k) * half : (slot(k) + 1) * half] for k in ends], axis=1)
+                    part = dot_tn(block, text_low[:, which * fold : (which + 1) * fold])
+                    for k in range(RING):
+                        if g == 0:
+                            i_own[which, k] = part[k * half : (k + 1) * half, :]
+                        else:
+                            i_tx[which, g, k] = part[k * half : (k + 1) * half, :].astype(BF16)
+                    if g > 0:
+                        push(i_tx.at[which, g], i_rx.at[which, RING - g], im_s, im_r.at[which, 0],
+                             along(1 - which, g))
 
         def image_second():
             for which in (0, 1):
-                for k in (1, 3, 2):
-                    arrived(i_rx.at[which, k], im_r.at[which, k])
+                arrived(i_rx.at[which, 1:RING], im_r.at[which, 0])
                 for g in (2, 1, 3, 0):
                     total = i_own[which, g]
                     for k in range(1, RING):
@@ -517,26 +498,23 @@
                     else:
                         i_st[which, g] = total.astype(BF16)
                         push(i_st.at[which, g], i_end.at[which, RING - g],
-                             im_s.at[which, RING + g], im_r.at[which, 2 * RING - g],
-                             along(which, g))
+                             im_s, im_r.at[which, 1], along(which, g))
 
         mine = tile(e, chunk)
 
         with jax.named_scope("j_weights"):
+            relay_weight(1, 1)
+            relay_weight(1, line - 1)
             slopes(cross)
-            index = far(2) * CORES + sib
-            arrived(wi_all.at[index], ww_r.at[0, index])
-            slopes(index)
-            for step in range(line):
-                index = far(step) * CORES + sib
-                arrived(wo_all.at[index], ww_r.at[1, index])
+            arrived(wi_all.at[0], ww_r.at[0, 3])
+            slopes(far(2) * CORES + sib)
+            arrived(wo_all.at[0:line], ww_r.at[1, 2])
 
         with jax.named_scope("i_topgrad"):
             total = join(spot)
-            for hop in hops[:-1]:
-                where = far(hop)
-                arrived(t_rx.at[where], tc_r.at[where])
-                total = total + t_rx[where].astype(F32)
+            arrived(t_rx.at[0 : line - 1], tc_r)
+            for k in range(line - 1):
+                total = total + t_rx[k].astype(F32)
             unit, length = unit_rows(text[mine, :])
             g_st[n_sec - 1] = unit_backward(unit, length, mult * total).astype(BF16)
 
@@ -546,28 +524,14 @@
 
                 @pl.when(spot != place)
                 def _():
-                    copy(g_st.at[layer], g_all.at[e], gs_s.at[layer, c], gs_r.at[e],
+                    copy(g_st.at[layer], g_all.at[e], gs_s, gs_r.at[e],
                          at(place, core)).start()
 
             @pl.when(s == layer)
             def _():
                 g_all[e] = g_st[layer]
-                copy(g_st.at[layer], g_all.at[e], gs_s.at[layer, chips], gs_r.at[e],
+                copy(g_st.at[layer], g_all.at[e], gs_s, gs_r.at[e],
                      at(spot, sib)).start()
-
-        def drain_spread(layer):
-            for c in range(chips):
-                place = layer * chips + c
-
-                @pl.when(spot != place)
-                def _():
-                    copy(g_st.at[layer], g_all.at[e], gs_s.at[layer, c], gs_r.at[e],
-                         at(place, core)).wait_send()
-
-            @pl.when(s == layer)
-            def _():
-                copy(g_st.at[layer], g_all.at[e], gs_s.at[layer, chips], gs_r.at[e],
-                     at(spot, sib)).wait_send()
 
         def feed_forward(layer):
             spread(layer)
@@ -599,14 +563,14 @@
             for hop in (1, 3, 2) if line == 4 else range(1, line):
                 index = far(hop) * CORES + core
                 arrived(g_all.at[index], gs_r.at[index])
-                push(g_all.at[index], g_all.at[index], gr_s.at[hop], gs_r.at[index],
+                push(g_all.at[index], g_all.at[index], gs_s, gs_r.at[index],
                      at(spot, sib))
                 weight_rows(index)
             input_out[mine, :] = in_st[s]
-            push(in_st.at[s], slab(e), in_s.at[0], in_r.at[e], at(spot, sib))
+            push(in_st.at[s], slab(e), in_s, in_r.at[0], at(spot, sib))
             for hop in hops[:-1]:
                 where = far(hop)
-                push(in_st.at[where // chips], slab(e), in_s.at[hop], in_r.at[e],
+                push(in_st.at[where // chips], slab(e), in_s, in_r.at[line - hop],
                      at(where, core))
             image_second()
             for hop in (0, 1, 3, 2) if line == 4 else range(line):
@@ -618,24 +582,24 @@
             for k in (2, 1, 3):
                 other = lax.rem(band[which] + k, RING)
                 push(w_tx.at[which, tile(other, RING * share), :], w_rx.at[which, RING - k],
-                     w_s.at[which, k], w_r.at[which, RING - k], along(1 - which, k))
+                     w_s, w_r.at[which, 0], along(1 - which, k))
 
         def weight_second(which):
             total = w_full[which, tile(band[which], RING * share), :]
+            arrived(w_rx.at[which, 1:RING], w_r.at[which, 0])
             for k in (1, 3, 2):
-                arrived(w_rx.at[which, k], w_r.at[which, k])
                 total = total + w_rx[which, k].astype(F32)
             w_sum[which] = total
             w_st[which] = total.astype(BF16)
             for k in (2, 1, 3):
                 other = lax.rem(band[1 - which] + k, RING)
                 push(w_st.at[which, tile(other, share), :], w_end.at[which, RING - k],
-                     w_s.at[which, RING + k], w_r.at[which, 2 * RING - k], along(which, k))
+                     w_s, w_r.at[which, 1], along(which, k))
 
         def weight_last(which, out):
             total = w_sum[which, tile(band[1 - which], share), :]
+            arrived(w_end.at[which, 1:RING], w_r.at[which, 1])
             for k in (1, 3, 2):
-                arrived(w_end.at[which, k], w_r.at[which, RING + k])
                 total = total + w_end[which, k].astype(F32)
             out[...] = total
 
@@ -656,22 +620,23 @@
         with jax.named_scope("q_image"):
             image_half = tile(s, half)
             unit, length = unit_rows(image[image_half, :])
+            sides = []
             for which in (0, 1):
                 total = i_own[which, 0]
+                arrived(i_end.at[which, 1:RING], im_r.at[which, 1])
                 for k in (1, 3, 2):
-                    arrived(i_end.at[which, k], im_r.at[which, RING + k])
                     total = total + i_end[which, k].astype(F32)
-                part = slice(which * fold, (which + 1) * fold)
-                image_out[tile(2 * s + which, fold), :] = unit_backward(
-                    unit[part, :], length[part, :], mult * total).astype(BF16)
+                sides.append(total)
+            image_out[image_half, :] = unit_backward(
+                unit, length, mult * jnp.concatenate(sides, axis=1)).astype(BF16)
             push(image_out.at[image_half, :], image_out.at[image_half, :], io_s, io_r,
                  {"section": 1 - s})
 
         with jax.named_scope("o_inrelay"):
             for hop in hops[:-1]:
                 index = far(hop) * CORES + core
-                arrived(slab(index), in_r.at[index])
-                push(slab(index), slab(index), ir_s.at[hop], in_r.at[index], at(spot, sib))
+                arrived(slab(index), in_r.at[hop])
+                push(slab(index), slab(index), in_s, in_r.at[0], at(spot, sib))
 
         with jax.named_scope("p_wsecond"):
             weight_second(1)
@@ -682,14 +647,22 @@
             weight_last(0, first_out)
 
         with jax.named_scope("r_drain"):
-            for step in range(line):
-                index = far(step) * CORES + sib
-                arrived(slab(index), in_r.at[index])
+            arrived(input_out.at[0 : line * chunk, :], in_r.at[0])
             arrived(image_out.at[tile(1 - s, half), :], io_r)
-            for c in sent + passed:
-                c.wait_send()
-            for layer in range(n_sec):
-                drain_spread(layer)
+            left(hidden.at[0:chunk, :], h_s)
+            left(cols.at[0 : 15 * half, :], gat_s)
+            left(col_rx.at[0 : n_dp - 1], cs_s)
+            left(row_rx.at[0 : n_el - 1], rs_s)
+            for which in (0, 1):
+                left(ww[which][1].at[0:6], ww_s.at[which])
+                left(ww[which][1].at[0], wc_s.at[which])
+            left(t_sx, ts_s)
+            left(t_tx.at[0 : line - 1], tc_s)
+            left(g_all.at[0 : 2 * n_sec + line - 1], gs_s)
+            left(input_out.at[0 : (2 * line - 1) * chunk, :], in_s)
+            left(text.at[0 : 2 * (RING - 1) * (RING + 1) * share, :], w_s)
+            left(cols.at[0 : 15 * half, :], im_s)
+            left(image_out.at[0:half, :], io_s)
 
     return kernel
 
@@ -758,27 +731,14 @@
                 pltpu.VMEM((2, RING * share, hid), F32),
                 pltpu.VMEM((2, RING * share, hid), BF16),
                 pltpu.VMEM((2, RING, share, hid), BF16),
-                pltpu.VMEM((2, RING, RING, half // 2, feats), BF16),
-                pltpu.VMEM((2, RING, RING, half // 2, feats), BF16),
-                pltpu.VMEM((2, RING, half // 2, feats), F32),
-                pltpu.VMEM((2, RING, half // 2, feats), BF16),
-                pltpu.VMEM((2, RING, half // 2, feats), BF16),
-                dma((44,)), dma((n_dp, 4)),
-                dma((n_dp,)), dma((n_dp,)),
-                dma((n_el,)), dma((n_el,)),
-                dma((2, 8)), dma((2, n_el + 5)),
-                dma, dma,
-                dma((line,)), dma((line,)),
-                dma((line,)), dma((line,)),
-                dma((n_sec, line + 1)), dma((n_el,)),
-                dma((line,)),
-                dma((line,)), dma((n_el,)),
-                dma((line,)),
-                dma((5,)),
-                dma((2, 2 * RING)), dma((2, 2 * RING)),
-                dma((2, 2 * RING)), dma((2, 2 * RING)),
-                dma((2, 2 * RING)), dma((2, 2 * RING)),
-                dma, dma,
+                pltpu.VMEM((2, RING, RING, half, feats // 2), BF16),
+                pltpu.VMEM((2, RING, RING, half, feats // 2), BF16),
+                pltpu.VMEM((2, RING, half, feats // 2), F32),
+                pltpu.VMEM((2, RING, half, feats // 2), BF16),
+                pltpu.VMEM((2, RING, half, feats // 2), BF16),
+                dma, dma((25,)), dma, dma, dma, dma, dma((2,)), dma((2, 4)), dma, dma,
+                dma, dma((line,)), dma, dma, dma, dma((n_el,)), dma, dma((line,)),
+                dma((5,)), dma((2,)), dma((2, 3)), dma, dma((2, 2)), dma, dma((2, 2)), dma, dma,
             ],
             compiler_params=pltpu.CompilerParams(
                 collective_id=0, has_side_effects=True, vmem_limit_bytes=57000000

time: 74.4 us -> 74.4 us (level); the launches traced: 74.3 us -> 73.6 us
  Pallas kernels: 72.9 us -> 72.1 us
    pallas_call x1, Pallas kernels: 71.9 us -> 71.2 us  [body(): pl.pallas_call(make_kernel(n_sec, n_dp, n_mp), out_shape=(pltpu.VMEM((own...]
where the time goes in v7:
time: 74.4 us; the launch traced here: 73.6 us
  Pallas kernels  72.1 us (97%)
  between operations  1.45 us (2%)
    pallas_call x1, Pallas kernels, body(): pl.pallas_call(make_kernel(n_sec, n_dp, n_mp), out_shape=(pltpu.VMEM((own...  71.2 us

profile of v7, /device:TPU:0, one launch (start us, length us, event | category | flops | bytes accessed | tf_op | source)
XLA Modules:
  0.0 73.6 jit_solution(604747786362407590)
XLA Ops:
  1.3 71.2 %shard_map.93 = (bf16[256,512]{1,0:T(8,128)(2,1)S(1)}, bf16[1024,256]{1,0:T(8,128)(2,1)S(1)}, f32[32,512]{1,0:T(8,128)S(1)}, f32[32,512]{1,0:T(8,128)S(1)}) custom-call(bf16[1024,512]{1,0:T(8,128)(2,1)} %text_hbm.1, bf16[256,512]{1,0:T(8,128)(2,1)} %image_hbm.1, f32[1]{0:T(128)S(6)} %copy.10.scale_ref, bf16[1024,512]{1,0:T(8,128)(2,1)} %bitcast.5, ...), custom_call_target="tpu_custom_call" | custom-call | tf_op jit(solution)/shard_map/pallas_call | solution.py:685
  72.5 0.9 %shard_map.94 = (bf16[256,512]{1,0:T(8,128)(2,1)}, bf16[1024,256]{1,0:T(8,128)(2,1)}, f32[32,512]{1,0:T(8,128)}, f32[32,512]{1,0:T(8,128)}) custom-call(bf16[256,512]{1,0:T(8,128)(2,1)S(1)} %get-tuple-element.12.refs_0_, bf16[1024,256]{1,0:T(8,128)(2,1)S(1)} %get-tuple-element.13.refs_1_, f32[32,512]{1,0:T(8,128)S(1)} %get-tuple-element.14.refs_2_, ...), custom_call_target="tpu_custom_call" | custom-call | tf_op jit(solution)/shard_map/pallas_call | solution.py:747

commit v8 on v7

--- a/solution.py
+++ b/solution.py
@@ -57,7 +57,7 @@
     def kernel(
         text_hbm, image_hbm, scale_ref, hidden_hbm, w_in_hbm, w_out_hbm,
         image_out, input_out, first_out, second_out,
-        text, image, hidden, text_low, cols, scores, sgrad, row_max, row_sum, row_lse, col_lse, row_st, row_rx, row_mix, col_st, col_rx,
+        text, image, hidden, text_low, cols, scores, sgrad, row_max, row_sum, row_part, col_lse, row_st, row_rx, row_mix, col_st, col_rx,
         wi_all, wo_all, h_own, t_full, t_keep, t_sx, t_sr, t_tx, t_rx,
         g_st, g_all, slope_own, in_st, act_all, slope_all, pre_all,
         w_full, w_tx, w_rx, w_sum, w_st, w_end, i_tx, i_rx, i_own, i_st, i_end,
@@ -414,29 +414,29 @@
             arrived(h_own.at[1 - s], h_r)
             for step in (0, 1, line - 1):
                 slopes(far(step) * CORES + core)
-            arrived(wi_all.at[0:3], ww_r.at[0, 2])
-            for step in (0, 1, line - 1):
-                slopes(far(step) * CORES + sib)
+
+        with jax.named_scope("f_rows"):
+            arrived(row_rx.at[0 : n_el - 1], rs_r)
+            row_mix[...] = merge(row_rx, n_el)
+            for r in range(n_el):
+                part = slice(r * chunk, (r + 1) * chunk)
+                place = far(hops[r // CORES]) * CORES + r % CORES
+                base = jnp.broadcast_to(row_mix[pl.ds(place, 1), :], (LANES, chunk)).T
+                for k in range(n_dp):
+                    row_part[k, part, :] = jnp.exp2(scores[k, part, :] - base)
 
         with jax.named_scope("f_merge"):
             arrived(col_rx.at[0 : n_dp - 1], cs_r)
             col_lse[...] = merge(col_rx, n_dp)
-            arrived(row_rx.at[0 : n_el - 1], rs_r)
-            row_mix[...] = merge(row_rx, n_el)
-            for r in range(n_el):
-                place = far(hops[r // CORES]) * CORES + r % CORES
-                row_lse[r * chunk : (r + 1) * chunk, :] = jnp.broadcast_to(
-                    row_mix[pl.ds(place, 1), :], (LANES, chunk)).T
 
         def score_rows(i):
             part = slice(i * pair, (i + 1) * pair)
-            base = row_lse[part, :]
             offset = (m - far(hops[i])) * pair + s * half
             for step in steps:
                 k = slot(step)
                 value = scores[k, part, :]
                 low = col_lse[pl.ds(shift(step), 1), :]
-                both = jnp.exp2(value - base) + jnp.exp2(value - low)
+                both = row_part[k, part, :] + jnp.exp2(value - low)
                 if k == 0:
                     diagonal = lax.broadcasted_iota(jnp.int32, (pair, half), 0) == (
                         lax.broadcasted_iota(jnp.int32, (pair, half), 1) + offset)
@@ -468,23 +468,29 @@
             cross_third(0)
             cross_third(1)
 
-        fold = feats // 2
+        fold = half // 2
 
         with jax.named_scope("h_image"):
             for g in (2, 1, 3, 0):
-                for which in (0, 1):
-                    ends = [(g, k) if which == 0 else (k, g) for k in range(RING)]
-                    block = jnp.concatenate(
-                        [sgrad[:, slot(k) * half : (slot(k) + 1) * half] for k in ends], axis=1)
-                    part = dot_tn(block, text_low[:, which * fold : (which + 1) * fold])
-                    for k in range(RING):
-                        if g == 0:
-                            i_own[which, k] = part[k * half : (k + 1) * half, :]
-                        else:
-                            i_tx[which, g, k] = part[k * half : (k + 1) * half, :].astype(BF16)
-                    if g > 0:
-                        push(i_tx.at[which, g], i_rx.at[which, RING - g], im_s, im_r.at[which, 0],
-                             along(1 - which, g))
+                part = dot_tn(sgrad[:, g * RING * half : (g + 1) * RING * half], text_low[...])
+                for k in range(RING):
+                    low = part[k * half : k * half + fold, :]
+                    high = part[k * half + fold : (k + 1) * half, :]
+                    if g == 0:
+                        i_own[0, k] = low
+                    else:
+                        i_tx[0, g, k] = low.astype(BF16)
+                    if k == 0:
+                        i_own[1, g] = high
+                    else:
+                        i_tx[1, k, g] = high.astype(BF16)
+                if g > 0:
+                    push(i_tx.at[0, g], i_rx.at[0, RING - g], im_s, im_r.at[0, 0], along(1, g))
+                if g == 1:
+                    relay_weight(1, 1)
+                    relay_weight(1, line - 1)
+            for k in (2, 1, 3):
+                push(i_tx.at[1, k], i_rx.at[1, RING - k], im_s, im_r.at[1, 0], along(0, k))
 
         def image_second():
             for which in (0, 1):
@@ -503,8 +509,9 @@
         mine = tile(e, chunk)
 
         with jax.named_scope("j_weights"):
-            relay_weight(1, 1)
-            relay_weight(1, line - 1)
+            arrived(wi_all.at[0:3], ww_r.at[0, 2])
+            for step in (0, 1, line - 1):
+                slopes(far(step) * CORES + sib)
             slopes(cross)
             arrived(wi_all.at[0], ww_r.at[0, 3])
             slopes(far(2) * CORES + sib)
@@ -519,13 +526,12 @@
             g_st[n_sec - 1] = unit_backward(unit, length, mult * total).astype(BF16)
 
         def spread(layer):
-            for c in range(chips):
-                place = layer * chips + c
-
-                @pl.when(spot != place)
+            for step in (2, 1, 3) if line == 4 else range(1, line):
+                place = far(step)
+
+                @pl.when(place // chips == layer)
                 def _():
-                    copy(g_st.at[layer], g_all.at[e], gs_s, gs_r.at[e],
-                         at(place, core)).start()
+                    copy(g_st.at[layer], g_all.at[e], gs_s, gs_r.at[e], at(place, core)).start()
 
             @pl.when(s == layer)
             def _():
@@ -535,12 +541,14 @@
 
         def feed_forward(layer):
             spread(layer)
+            first = layer * n_mp
             total = g_st[layer].astype(F32)
+            grads = []
             for j in range(n_mp):
-                index = layer * n_mp + j
-                back = dot_nt(g_st[layer], wo_all[index])
-                grad = (back * slope_own[index]).astype(BF16)
-                total = total + dot_nt(grad, wi_all[index])
+                back = dot_nt(g_st[layer], wo_all[first + j])
+                grads.append((back * slope_own[first + j]).astype(BF16))
+            for j in range(n_mp):
+                total = total + dot_nt(grads[j], wi_all[first + j])
             if layer > 0:
                 g_st[layer - 1] = total.astype(BF16)
             else:
@@ -620,15 +628,14 @@
         with jax.named_scope("q_image"):
             image_half = tile(s, half)
             unit, length = unit_rows(image[image_half, :])
-            sides = []
             for which in (0, 1):
                 total = i_own[which, 0]
                 arrived(i_end.at[which, 1:RING], im_r.at[which, 1])
                 for k in (1, 3, 2):
                     total = total + i_end[which, k].astype(F32)
-                sides.append(total)
-            image_out[image_half, :] = unit_backward(
-                unit, length, mult * jnp.concatenate(sides, axis=1)).astype(BF16)
+                part = slice(which * fold, (which + 1) * fold)
+                image_out[tile(2 * s + which, fold), :] = unit_backward(
+                    unit[part, :], length[part, :], mult * total).astype(BF16)
             push(image_out.at[image_half, :], image_out.at[image_half, :], io_s, io_r,
                  {"section": 1 - s})
 
@@ -702,7 +709,7 @@
                 pltpu.VMEM((rows, columns), BF16),
                 pltpu.VMEM((rows, LANES), F32),
                 pltpu.VMEM((rows, LANES), F32),
-                pltpu.VMEM((rows, LANES), F32),
+                pltpu.VMEM((n_dp, rows, half), F32),
                 pltpu.VMEM((n_dp, half), F32),
                 pltpu.VMEM((n_el, chunk), F32),
                 pltpu.VMEM((n_el, n_el, chunk), F32),
@@ -731,17 +738,17 @@
                 pltpu.VMEM((2, RING * share, hid), F32),
                 pltpu.VMEM((2, RING * share, hid), BF16),
                 pltpu.VMEM((2, RING, share, hid), BF16),
-                pltpu.VMEM((2, RING, RING, half, feats // 2), BF16),
-                pltpu.VMEM((2, RING, RING, half, feats // 2), BF16),
-                pltpu.VMEM((2, RING, half, feats // 2), F32),
-                pltpu.VMEM((2, RING, half, feats // 2), BF16),
-                pltpu.VMEM((2, RING, half, feats // 2), BF16),
+                pltpu.VMEM((2, RING, RING, half // 2, feats), BF16),
+                pltpu.VMEM((2, RING, RING, half // 2, feats), BF16),
+                pltpu.VMEM((2, RING, half // 2, feats), F32),
+                pltpu.VMEM((2, RING, half // 2, feats), BF16),
+                pltpu.VMEM((2, RING, half // 2, feats), BF16),
                 dma, dma((25,)), dma, dma, dma, dma, dma((2,)), dma((2, 4)), dma, dma,
                 dma, dma((line,)), dma, dma, dma, dma((n_el,)), dma, dma((line,)),
                 dma((5,)), dma((2,)), dma((2, 3)), dma, dma((2, 2)), dma, dma((2, 2)), dma, dma,
             ],
             compiler_params=pltpu.CompilerParams(
-                collective_id=0, has_side_effects=True, vmem_limit_bytes=57000000
+                collective_id=0, has_side_effects=True, vmem_limit_bytes=62000000
             ),
         )(text, image, scale, hidden[0], w_in[0], w_out[0])
         image_grad, input_grad, first, second = pl.pallas_call(

time: 74.4 us -> 71.7 us (0.964)
  Pallas kernels: 72.1 us -> 69.4 us
    pallas_call x1, Pallas kernels: 71.2 us -> 68.5 us  [body(): pl.pallas_call(make_kernel(n_sec, n_dp, n_mp), out_shape=(pltpu.VMEM((own...]
where the time goes in v8:
time: 71.7 us; the launch traced here: 70.9 us
  Pallas kernels  69.4 us (97%)
  between operations  1.45 us (2%)
    pallas_call x1, Pallas kernels, body(): pl.pallas_call(make_kernel(n_sec, n_dp, n_mp), out_shape=(pltpu.VMEM((own...  68.5 us

profile of v8, /device:TPU:0, one launch (start us, length us, event | category | flops | bytes accessed | tf_op | source)
XLA Modules:
  0.0 70.9 jit_solution(5673443285526712945)
XLA Ops:
  1.3 68.5 %shard_map.93 = (bf16[256,512]{1,0:T(8,128)(2,1)S(1)}, bf16[1024,256]{1,0:T(8,128)(2,1)S(1)}, f32[32,512]{1,0:T(8,128)S(1)}, f32[32,512]{1,0:T(8,128)S(1)}) custom-call(bf16[1024,512]{1,0:T(8,128)(2,1)} %text_hbm.1, bf16[256,512]{1,0:T(8,128)(2,1)} %image_hbm.1, f32[1]{0:T(128)S(6)} %copy.10.scale_ref, bf16[1024,512]{1,0:T(8,128)(2,1)} %bitcast.5, ...), custom_call_target="tpu_custom_call" | custom-call | tf_op jit(solution)/shard_map/pallas_call | solution.py:692
  69.7 0.9 %shard_map.94 = (bf16[256,512]{1,0:T(8,128)(2,1)}, bf16[1024,256]{1,0:T(8,128)(2,1)}, f32[32,512]{1,0:T(8,128)}, f32[32,512]{1,0:T(8,128)}) custom-call(bf16[256,512]{1,0:T(8,128)(2,1)S(1)} %get-tuple-element.12.refs_0_, bf16[1024,256]{1,0:T(8,128)(2,1)S(1)} %get-tuple-element.13.refs_1_, f32[32,512]{1,0:T(8,128)S(1)} %get-tuple-element.14.refs_2_, ...), custom_call_target="tpu_custom_call" | custom-call | tf_op jit(solution)/shard_map/pallas_call | solution.py:754

commit v9 on v8

--- a/solution.py
+++ b/solution.py
@@ -217,19 +217,22 @@
             part = tile(cell[which], bit)
             push(ww[which][0].at[part, :], ww[which][1].at[e, part, :], wc_s.at[which],
                  wc_r.at[which, 0], at(far(2), core))
-        top = pl.ds(0, w_in.shape[0] // 2)
-        rest = pl.ds(w_in.shape[0] // 2, w_in.shape[0] // 2)
+        depth = w_in.shape[0]
+        whole = (pl.ds(0, depth // 2), pl.ds(depth // 2, depth // 2))
+        early = (pl.ds(0, depth // 4),)
+        later = (pl.ds(depth // 4, depth // 4), pl.ds(depth // 2, depth // 2))
 
         def neighbour(which, toward, part):
             push(ww[which][0].at[part, :], ww[which][1].at[e, part, :], ww_s.at[which],
                  ww_r.at[which, 1 if toward == 1 else 0], at(far(toward), core))
 
-        def both_ways(which):
-            for part in (top, rest):
+        def both_ways(which, parts):
+            for part in parts:
                 neighbour(which, line - 1, part)
                 neighbour(which, 1, part)
 
-        both_ways(0)
+        both_ways(0, whole)
+        both_ways(1, early)
 
         for which in (0, 1):
             push(ww[which][0], ww[which][1].at[e], ww_s.at[which], ww_r.at[which, 2],
@@ -318,16 +321,16 @@
         with jax.named_scope("c_blocks"):
             landed((0, 1), "A")
             forward((0, 1), "A0", "Y-")
-            forward((0, 1), "A", "Z-", "Z+")
             landed((1, 0), "B")
             forward((1, 0), "B0", "Z-")
-            forward((1, 0), "B", "Y-", "Y+")
             landed((0, 3), "A")
             forward((0, 3), "A1", "Y+")
-            forward((0, 3), "A", "Z-", "Z+")
             landed((3, 0), "B")
             forward((3, 0), "B1", "Z+")
-            forward((3, 0), "B", "Y-", "Y+")
+            for dy in (1, 3):
+                forward((0, dy), "A", "Z-", "Z+")
+            for dz in (1, 3):
+                forward((dz, 0), "B", "Y-", "Y+")
             landed((0, 1), "B")
             forward((0, 1), "B0", "Y-")
             landed((1, 0), "A")
@@ -390,7 +393,7 @@
             for q in others(e, n_el):
                 push(row_st, row_rx.at[e], rs_s, rs_r,
                      {"section": q // n_mp, "mp": lax.rem(q, n_mp)})
-            both_ways(1)
+            both_ways(1, later)
 
         def merge(rx, count):
             peak = rx[0]
@@ -486,11 +489,12 @@
                         i_tx[1, k, g] = high.astype(BF16)
                 if g > 0:
                     push(i_tx.at[0, g], i_rx.at[0, RING - g], im_s, im_r.at[0, 0], along(1, g))
+                for k in (2, 1, 3):
+                    push(i_tx.at[1, k, g], i_rx.at[1, RING - k, g], im_s, im_r.at[1, 0],
+                         along(0, k))
                 if g == 1:
                     relay_weight(1, 1)
                     relay_weight(1, line - 1)
-            for k in (2, 1, 3):
-                push(i_tx.at[1, k], i_rx.at[1, RING - k], im_s, im_r.at[1, 0], along(0, k))
 
         def image_second():
             for which in (0, 1):

time: 71.7 us -> 71.4 us (level)
  no operation moved by 1% of the time
where the time goes in v9:
time: 71.4 us; the launch traced here: 71.1 us
  Pallas kernels  69.6 us (97%)
  between operations  1.45 us (2%)
    pallas_call x1, Pallas kernels, body(): pl.pallas_call(make_kernel(n_sec, n_dp, n_mp), out_shape=(pltpu.VMEM((own...  68.7 us

profile of v9, /device:TPU:0, one launch (start us, length us, event | category | flops | bytes accessed | tf_op | source)
XLA Modules:
  0.0 71.1 jit_solution(4027136410814234678)
XLA Ops:
  1.3 68.7 %shard_map.93 = (bf16[256,512]{1,0:T(8,128)(2,1)S(1)}, bf16[1024,256]{1,0:T(8,128)(2,1)S(1)}, f32[32,512]{1,0:T(8,128)S(1)}, f32[32,512]{1,0:T(8,128)S(1)}) custom-call(bf16[1024,512]{1,0:T(8,128)(2,1)} %text_hbm.1, bf16[256,512]{1,0:T(8,128)(2,1)} %image_hbm.1, f32[1]{0:T(128)S(6)} %copy.10.scale_ref, bf16[1024,512]{1,0:T(8,128)(2,1)} %bitcast.5, ...), custom_call_target="tpu_custom_call" | custom-call | tf_op jit(solution)/shard_map/pallas_call | solution.py:696
  70.0 0.9 %shard_map.94 = (bf16[256,512]{1,0:T(8,128)(2,1)}, bf16[1024,256]{1,0:T(8,128)(2,1)}, f32[32,512]{1,0:T(8,128)}, f32[32,512]{1,0:T(8,128)}) custom-call(bf16[256,512]{1,0:T(8,128)(2,1)S(1)} %get-tuple-element.12.refs_0_, bf16[1024,256]{1,0:T(8,128)(2,1)S(1)} %get-tuple-element.13.refs_1_, f32[32,512]{1,0:T(8,128)S(1)} %get-tuple-element.14.refs_2_, ...), custom_call_target="tpu_custom_call" | custom-call | tf_op jit(solution)/shard_map/pallas_call | solution.py:758

commit v10 on v9

--- a/solution.py
+++ b/solution.py
@@ -55,9 +55,9 @@
     n_el = n_sec * n_mp
 
     def kernel(
-        text_hbm, image_hbm, scale_ref, hidden_hbm, w_in_hbm, w_out_hbm,
+        text_hbm, image_hbm, scale_hbm, hidden_hbm, w_in_hbm, w_out_hbm,
         image_out, input_out, first_out, second_out,
-        text, image, hidden, text_low, cols, scores, sgrad, row_max, row_sum, row_part, col_lse, row_st, row_rx, row_mix, col_st, col_rx,
+        scale_ref, text, image, hidden, text_low, cols, scores, sgrad, row_max, row_sum, row_part, col_lse, row_st, row_rx, row_mix, col_st, col_rx,
         wi_all, wo_all, h_own, t_full, t_keep, t_sx, t_sr, t_tx, t_rx,
         g_st, g_all, slope_own, in_st, act_all, slope_all, pre_all,
         w_full, w_tx, w_rx, w_sum, w_st, w_end, i_tx, i_rx, i_own, i_st, i_end,
@@ -69,14 +69,12 @@
         d = lax.axis_index("dp")
         m = lax.axis_index("mp")
         rows, feats = text.shape
-        own = image.shape[0]
+        own = image_hbm.shape[0]
         half = own // n_sec
         chunk = rows // n_el
         pair = rows // line
         share = feats // n_dp
         width = feats // n_sec
-        mult = scale_ref[0]
-        mult2 = mult * LOG2E
         core = lax.rem(m, CORES)
         sib = 1 - core
         spot = s * chips + m // CORES
@@ -128,8 +126,8 @@
             loads = [
                 pltpu.make_async_copy(src, dst, ld_s.at[k])
                 for k, (src, dst) in enumerate((
-                    (image_hbm, image), (text_hbm, text), (hidden_hbm, hidden),
-                    (w_in_hbm, wi_all.at[e]), (w_out_hbm, wo_all.at[e]),
+                    (image_hbm.at[tile(s, half), :], image), (text_hbm, text), (hidden_hbm, hidden),
+                    (w_in_hbm, wi_all.at[e]), (w_out_hbm, wo_all.at[e]), (scale_hbm, scale_ref),
                 ))
             ]
             for load in loads:
@@ -144,7 +142,7 @@
                     device_id_type=MESH,
                 )
             loads[0].wait()
-            own_unit, _ = unit_rows(image[tile(s, half), :])
+            own_unit, _ = unit_rows(image[...])
             cols[0:half, :] = own_unit.astype(BF16)
             pl.semaphore_wait(barrier, n_el + 3)
 
@@ -199,6 +197,8 @@
 
         for load in loads[2:]:
             load.wait()
+        mult = scale_ref[0]
+        mult2 = mult * LOG2E
         h_own[s] = hidden[tile(e, chunk), :]
         mate = (1 - s) * n_mp + m
         push(hidden.at[tile(mate, chunk), :], h_own.at[s], h_s, h_r, {"section": 1 - s})
@@ -544,7 +544,6 @@
                      at(spot, sib)).start()
 
         def feed_forward(layer):
-            spread(layer)
             first = layer * n_mp
             total = g_st[layer].astype(F32)
             grads = []
@@ -555,6 +554,7 @@
                 total = total + dot_nt(grads[j], wi_all[first + j])
             if layer > 0:
                 g_st[layer - 1] = total.astype(BF16)
+                spread(layer - 1)
             else:
                 for t in range(n_sec):
                     in_st[t] = total[:, t * width : (t + 1) * width].astype(BF16)
@@ -565,6 +565,8 @@
         with jax.named_scope("k_ffn"):
             for layer in range(n_sec - 1, -1, -1):
                 feed_forward(layer)
+                if layer == n_sec - 1:
+                    spread(layer)
 
         def weight_rows(k):
             back = dot_nt(g_all[k], w_out[...])
@@ -631,7 +633,7 @@
 
         with jax.named_scope("q_image"):
             image_half = tile(s, half)
-            unit, length = unit_rows(image[image_half, :])
+            unit, length = unit_rows(image[...])
             for which in (0, 1):
                 total = i_own[which, 0]
                 arrived(i_end.at[which, 1:RING], im_r.at[which, 1])
@@ -701,11 +703,12 @@
                 pltpu.VMEM((share, hid), F32),
                 pltpu.VMEM((share, hid), F32),
             ),
-            in_specs=[hbm, hbm, pl.BlockSpec(memory_space=pltpu.SMEM), hbm, hbm, hbm],
+            in_specs=[hbm, hbm, hbm, hbm, hbm, hbm],
             out_specs=(vmem,) * 4,
             scratch_shapes=[
+                pltpu.SMEM((1,), F32),
                 pltpu.VMEM((rows, feats), BF16),
-                pltpu.VMEM((own, feats), BF16),
+                pltpu.VMEM((half, feats), BF16),
                 pltpu.VMEM((rows, feats), BF16),
                 pltpu.VMEM((rows, feats), BF16),
                 pltpu.VMEM((columns, feats), BF16),
@@ -749,7 +752,7 @@
                 pltpu.VMEM((2, RING, half // 2, feats), BF16),
                 dma, dma((25,)), dma, dma, dma, dma, dma((2,)), dma((2, 4)), dma, dma,
                 dma, dma((line,)), dma, dma, dma, dma((n_el,)), dma, dma((line,)),
-                dma((5,)), dma((2,)), dma((2, 3)), dma, dma((2, 2)), dma, dma((2, 2)), dma, dma,
+                dma((6,)), dma((2,)), dma((2, 3)), dma, dma((2, 2)), dma, dma((2, 2)), dma, dma,
             ],
             compiler_params=pltpu.CompilerParams(
                 collective_id=0, has_side_effects=True, vmem_limit_bytes=62000000

time: 71.4 us -> 71.1 us (level)
  no operation moved by 1% of the time
where the time goes in v10:
time: 71.1 us; the launch traced here: 70.7 us
  Pallas kernels  69.3 us (97%)
  between operations  1.45 us (2%)
    pallas_call x1, Pallas kernels, body(): pl.pallas_call(make_kernel(n_sec, n_dp, n_mp), out_shape=(pltpu.VMEM((own...  68.3 us

profile of v10, /device:TPU:0, one launch (start us, length us, event | category | flops | bytes accessed | tf_op | source)
XLA Modules:
  0.0 70.7 jit_solution(12921219649086431500)
XLA Ops:
  1.3 68.3 %shard_map.93 = (bf16[256,512]{1,0:T(8,128)(2,1)S(1)}, bf16[1024,256]{1,0:T(8,128)(2,1)S(1)}, f32[32,512]{1,0:T(8,128)S(1)}, f32[32,512]{1,0:T(8,128)S(1)}) custom-call(bf16[1024,512]{1,0:T(8,128)(2,1)} %text_hbm.1, bf16[256,512]{1,0:T(8,128)(2,1)} %image_hbm.1, f32[1]{0:T(128)S(6)} %copy.10.scale_hbm, bf16[1024,512]{1,0:T(8,128)(2,1)} %bitcast.5, ...), custom_call_target="tpu_custom_call" | custom-call | tf_op jit(solution)/shard_map/pallas_call | solution.py:698
  69.6 0.9 %shard_map.94 = (bf16[256,512]{1,0:T(8,128)(2,1)}, bf16[1024,256]{1,0:T(8,128)(2,1)}, f32[32,512]{1,0:T(8,128)}, f32[32,512]{1,0:T(8,128)}) custom-call(bf16[256,512]{1,0:T(8,128)(2,1)S(1)} %get-tuple-element.12.refs_0_, bf16[1024,256]{1,0:T(8,128)(2,1)S(1)} %get-tuple-element.13.refs_1_, f32[32,512]{1,0:T(8,128)S(1)} %get-tuple-element.14.refs_2_, ...), custom_call_target="tpu_custom_call" | custom-call | tf_op jit(solution)/shard_map/pallas_call | solution.py:761

commit v11 on v10

--- a/solution.py
+++ b/solution.py
@@ -572,8 +572,17 @@
             back = dot_nt(g_all[k], w_out[...])
             pre_all[tile(k, chunk), :] = (back * slope_all[tile(k, chunk), :]).astype(BF16)
 
+        def some_rows(steps, who):
+            places = [far(step) * CORES + who for step in steps]
+            g_rows = jnp.concatenate([g_all[k] for k in places], axis=0)
+            act = jnp.concatenate([act_all[tile(k, chunk), :] for k in places], axis=0)
+            hid_rows = jnp.concatenate([hidden[tile(k, chunk), :] for k in places], axis=0)
+            pre = jnp.concatenate([pre_all[tile(k, chunk), :] for k in places], axis=0)
+            return (lambda: dot_tn(hid_rows, pre), lambda: dot_tn(g_rows, act))
+
         with jax.named_scope("m_weightrows"):
             weight_rows(e)
+            image_second()
             for hop in (1, 3, 2) if line == 4 else range(1, line):
                 index = far(hop) * CORES + core
                 arrived(g_all.at[index], gs_r.at[index])
@@ -586,7 +595,9 @@
                 where = far(hop)
                 push(in_st.at[where // chips], slab(e), in_s, in_r.at[line - hop],
                      at(where, core))
-            image_second()
+            ours = some_rows(range(line), core)
+            for which in (1, 0):
+                w_full[which] = ours[which]()
             for hop in (0, 1, 3, 2) if line == 4 else range(line):
                 index = far(hop) * CORES + sib
                 arrived(g_all.at[index], gs_r.at[index])
@@ -618,15 +629,15 @@
             out[...] = total
 
         with jax.named_scope("n_wgrad"):
-            g_rows = g_all[...].reshape(rows, feats)
-            grad = dot_tn(g_rows, act_all[...])
+            theirs = some_rows(range(line), sib)
+            grad = w_full[1] + theirs[1]()
             for p in range(n_dp):
                 q = (p % RING) * RING + p // RING
                 w_full[1, q * share : (q + 1) * share, :] = grad[p * share : (p + 1) * share, :]
                 w_tx[1, q * share : (q + 1) * share, :] = grad[
                     p * share : (p + 1) * share, :].astype(BF16)
             send_weights(1)
-            grad = dot_tn(hidden[...], pre_all[...])
+            grad = w_full[0] + theirs[0]()
             w_full[0] = grad
             w_tx[0] = grad.astype(BF16)
             send_weights(0)

time: 71.1 us -> 70.6 us (level)
  no operation moved by 1% of the time
where the time goes in v11:
time: 70.6 us; the launch traced here: 70.2 us
  Pallas kernels  68.8 us (97%)
  between operations  1.45 us (2%)
    pallas_call x1, Pallas kernels, body(): pl.pallas_call(make_kernel(n_sec, n_dp, n_mp), out_shape=(pltpu.VMEM((own...  67.8 us

profile of v11, /device:TPU:0, one launch (start us, length us, event | category | flops | bytes accessed | tf_op | source)
XLA Modules:
  0.0 70.2 jit_solution(14615482290981594272)
XLA Ops:
  1.3 67.8 %shard_map.93 = (bf16[256,512]{1,0:T(8,128)(2,1)S(1)}, bf16[1024,256]{1,0:T(8,128)(2,1)S(1)}, f32[32,512]{1,0:T(8,128)S(1)}, f32[32,512]{1,0:T(8,128)S(1)}) custom-call(bf16[1024,512]{1,0:T(8,128)(2,1)} %text_hbm.1, bf16[256,512]{1,0:T(8,128)(2,1)} %image_hbm.1, f32[1]{0:T(128)S(6)} %copy.10.scale_hbm, bf16[1024,512]{1,0:T(8,128)(2,1)} %bitcast.5, ...), custom_call_target="tpu_custom_call" | custom-call | tf_op jit(solution)/shard_map/pallas_call | solution.py:709
  69.1 0.9 %shard_map.94 = (bf16[256,512]{1,0:T(8,128)(2,1)}, bf16[1024,256]{1,0:T(8,128)(2,1)}, f32[32,512]{1,0:T(8,128)}, f32[32,512]{1,0:T(8,128)}) custom-call(bf16[256,512]{1,0:T(8,128)(2,1)S(1)} %get-tuple-element.12.refs_0_, bf16[1024,256]{1,0:T(8,128)(2,1)S(1)} %get-tuple-element.13.refs_1_, f32[32,512]{1,0:T(8,128)S(1)} %get-tuple-element.14.refs_2_, ...), custom_call_target="tpu_custom_call" | custom-call | tf_op jit(solution)/shard_map/pallas_call | solution.py:772
